TPU v7x, 32 devices: a whole 2x2x4 slice. The times are simulated.
32 devices in a mesh: groups: 2 (over x), frame: 8 (over z, y), band: 2 (over core).
Axes of the slice: x: 2, y: 2, z: 4, core: 2. Of those that a mesh axis runs over, the one named last changes fastest.
Arguments:
- hidden_in: bfloat16 [16, 1536, 1152], P(('groups', 'frame'), 'band'), parts along dimension 0, may hold values from -6 to 6
- latents: float32 [16, 192, 128], P(('groups', 'frame'), 'band'), parts along dimension 0, may hold values from -6 to 6
- fresh_noise: float32 [384, 128], P(('groups', 'band')), parts along dimension 0, may hold values from -6 to 6
- level_index: int32 [16], P(('groups', 'frame')), parts along dimension 0, may hold values from 1 to 31
- time_table: int32 [32], replicated, may hold values from 0 to 999, as said below
- frame_offset: int32 [2], P('groups'), parts along dimension 0, may hold values from 0 to 1023
- mod_table: float32 [3456], replicated, may hold values from -3 to 3
- time_weight: bfloat16 [128, 3456], replicated, may hold values from -0.5 to 0.5
- spatial_qkv: bfloat16 [1152, 1728], replicated, may hold values from -6 to 6
- spatial_out: bfloat16 [576, 1152], replicated, may hold values from -0.25 to 0.25
- temporal_qkv: bfloat16 [1152, 1728], replicated, may hold values from -6 to 6
- temporal_out: bfloat16 [576, 1152], replicated, may hold values from -0.25 to 0.25
- final_gain: float32 [1152], replicated, may hold values from 0.5 to 1.5
- out_weight: bfloat16 [1152, 16], replicated, may hold values from -0.1875 to 0.1875
Outputs:
- hidden_out: bfloat16 [16, 1536, 1152], P(('groups', 'frame'), 'band'), parts along dimension 0
- velocity: float32 [16, 192, 128], P(('groups', 'frame'), 'band'), parts along dimension 0
- next_latents: float32 [16, 192, 128], P(('groups', 'frame'), 'band'), parts along dimension 0
There are 2 independent parts, one for each index of `groups`. A program takes and returns all parts, laid end to end along the dimension named above; an argument that names none is the same for every part. Nothing has to cross between parts.
Inputs may be any that keep to these rules, and one draw needn't show every extreme that they name: `time_table`: entries rise strictly along the table, from 0 at the first entry to 999 at the last.
All inputs are finite; a program needn't handle non-finite values.
Results may differ from a plain program's by a relative error of at most 0.025.
Values may be sent and summed in bfloat16 or wider, within the bound.
No kernel may reach another device: no remote copies, remote signals or barrier semaphores. Data moves between devices by JAX's collectives and lax.ppermute only.
A program may use at most 128 MiB of HBM per device.

v0:
```python
import math

import jax
import jax.numpy as jnp
from jax import lax
from jax.sharding import PartitionSpec as P

HEAD_SIZE = 72


epsilon = 1e-06


def from_behind(value, axis, steps):
    count = lax.axis_size(axis)
    initial, last = (max(0, -steps), min(count, count - steps))
    return lax.ppermute(value, axis, [(source, source + steps) for source in range(initial, last)])


def layer_norm(values):
    average = jnp.mean(values, axis=-1, keepdims=True)
    centred = values - average
    variance = jnp.mean(centred * centred, axis=-1, keepdims=True)
    return centred * lax.rsqrt(variance + epsilon)


def sinusoid(position, feature_count, first_sine):
    half_width = feature_count // 2
    frequency = jnp.exp(-math.log(10000.0) * jnp.arange(half_width, dtype=jnp.float32) / half_width)
    angles = position.astype(jnp.float32)[:, None] * frequency[None, :]
    if first_sine:
        return jnp.concatenate([jnp.sin(angles), jnp.cos(angles)], axis=-1)
    return jnp.concatenate([jnp.cos(angles), jnp.sin(angles)], axis=-1)


def mix_frames(rows, head_count):
    frame_count = rows.shape[0]
    item_count = rows.shape[1]
    parted = rows.reshape(frame_count, item_count, 3, head_count, HEAD_SIZE)
    attention_scores = jnp.einsum(
        "fnhd,gnhd->nhfg", parted[:, :, 0], parted[:, :, 1], preferred_element_type=jnp.float32
    ) / math.sqrt(HEAD_SIZE)
    row_max = jnp.max(attention_scores, axis=-1, keepdims=True)
    attention_weight = jnp.exp(attention_scores - row_max).astype(jnp.bfloat16)
    denominator = jnp.sum(attention_weight, axis=-1, dtype=jnp.float32)
    weighted_sum = jnp.einsum(
        "nhfg,gnhd->fnhd", attention_weight, parted[:, :, 2], preferred_element_type=jnp.float32
    )
    mixed = weighted_sum / jnp.transpose(denominator, (2, 0, 1))[..., None]
    return mixed.astype(jnp.bfloat16).reshape(frame_count, item_count, head_count * HEAD_SIZE)


def body(
    hidden_in,
    latents,
    fresh_noise,
    level_index,
    time_table,
    frame_offset,
    mod_table,
    time_weight,
    spatial_qkv,
    spatial_out,
    temporal_qkv,
    temporal_out,
    final_gain,
    out_weight,
):
    tokens = hidden_in.shape[1]
    model_width = hidden_in.shape[2]
    attended = spatial_out.shape[0]
    head_count = attended // HEAD_SIZE
    peers = lax.axis_size("frame")
    table_index = jnp.arange(time_table.shape[0], dtype=jnp.int32)
    now_steps = jnp.sum(
        jnp.where(table_index[None, :] == level_index[:, None], time_table[None, :], 0), axis=1
    )
    next_steps = jnp.sum(
        jnp.where(table_index[None, :] == level_index[:, None] - 1, time_table[None, :], 0), axis=1
    )
    activated = jax.nn.silu(sinusoid(now_steps, time_weight.shape[0], False)).astype(jnp.bfloat16)
    modulation = mod_table[None, :] + jnp.dot(
        activated, time_weight, preferred_element_type=jnp.float32
    )
    shift_part = modulation[:, :model_width]
    scale_part = modulation[:, model_width : 2 * model_width]
    gate_part = modulation[:, 2 * model_width :]
    inputs = hidden_in[0].astype(jnp.float32)
    normed = (layer_norm(inputs) * (1.0 + scale_part) + shift_part).astype(jnp.bfloat16)
    projected = jnp.dot(normed, spatial_qkv, preferred_element_type=jnp.float32).astype(
        jnp.bfloat16
    )
    query_rows = projected[:, :attended].reshape(tokens, head_count, HEAD_SIZE)
    key_value = projected[:, attended:]
    block_rows = lax.all_gather(key_value, "band", axis=0, tiled=True)
    row_max = jnp.full((head_count, tokens), -1e30, jnp.float32)
    row_count = block_rows.shape[0]
    key_matrix_rows = block_rows[:, :attended].reshape(row_count, head_count, HEAD_SIZE)
    value_matrix_rows = block_rows[:, attended:].reshape(row_count, head_count, HEAD_SIZE)
    attention_scores = jnp.einsum(
        "ubg,wbg->buw", query_rows, key_matrix_rows, preferred_element_type=jnp.float32
    ) / math.sqrt(HEAD_SIZE)
    new_max = jnp.maximum(row_max, jnp.max(attention_scores, axis=-1))
    attention_weight = jnp.exp(attention_scores - new_max[:, :, None]).astype(jnp.bfloat16)
    denominator = jnp.sum(attention_weight, axis=-1, dtype=jnp.float32)
    weighted_sum = jnp.einsum(
        "leq,qlr->ler", attention_weight, value_matrix_rows, preferred_element_type=jnp.float32
    )
    row_max, denominator, weighted_sum = (new_max, denominator, weighted_sum)
    spatial_mixed = (
        jnp.transpose(weighted_sum / denominator[:, :, None], (1, 0, 2))
        .reshape(tokens, attended)
        .astype(jnp.bfloat16)
    )
    residual = inputs + gate_part * jnp.dot(
        spatial_mixed, spatial_out, preferred_element_type=jnp.float32
    )
    position = lax.axis_index("frame") + frame_offset
    placed = sinusoid(position, model_width, True)
    temporal_in = (residual + placed).astype(jnp.bfloat16)
    spread_rows = temporal_in.reshape(1, peers, tokens // peers, model_width)
    gathered = lax.all_to_all(spread_rows, "frame", split_axis=1, concat_axis=0, tiled=True)
    frame_count = gathered.shape[0]
    item_count = gathered.shape[2]
    rows = jnp.dot(
        gathered.reshape(frame_count * item_count, model_width),
        temporal_qkv,
        preferred_element_type=jnp.float32,
    ).astype(jnp.bfloat16)
    mixed = mix_frames(rows.reshape(frame_count, item_count, 3 * attended), head_count)
    mixed_rows = mixed.reshape(frame_count, 1, item_count, attended)
    mixed_pairs = mixed_rows.reshape(mixed_rows.shape[0], 1, mixed_rows.shape[2] // 2, 2 * attended)
    returned = lax.all_to_all(mixed_pairs, "frame", split_axis=0, concat_axis=1, tiled=True)
    temporal_mixed = returned.reshape(tokens, attended)
    residual = residual + gate_part * jnp.dot(
        temporal_mixed, temporal_out, preferred_element_type=jnp.float32
    )
    hidden_out = residual.astype(jnp.bfloat16)[None]
    final_rows = (layer_norm(residual) * final_gain).astype(jnp.bfloat16)
    velocity = jnp.dot(final_rows, out_weight, preferred_element_type=jnp.float32).reshape(
        1, latents.shape[1], 128
    )
    time_delta = (next_steps - now_steps).astype(jnp.float32) / 1000.0
    update = latents + time_delta[:, None, None] * velocity
    shifted = from_behind(update.astype(jnp.bfloat16), "frame", 1).astype(update.dtype)
    next_latents = jnp.where(lax.axis_index("frame") == 0, fresh_noise[None], shifted)
    return (hidden_out, velocity, next_latents)


def solution(mesh):
    placed = (
        P(("groups", "frame"), "band", None),
        P(("groups", "frame"), "band", None),
        P(("groups", "band"), None),
        P(("groups", "frame")),
        P(),
        P("groups"),
        P(),
        P(),
        P(),
        P(),
        P(),
        P(),
        P(),
        P(),
    )
    return jax.shard_map(
        body,
        mesh=mesh,
        in_specs=placed,
        out_specs=(
            P(("groups", "frame"), "band", None),
            P(("groups", "frame"), "band", None),
            P(("groups", "frame"), "band", None),
        ),
        check_vma=False,
    )
```

profile of v0, /device:TPU:0, one launch (start us, length us, event | category | flops | bytes accessed | tf_op | source)
XLA Modules:
  0.0 232.9 jit_solution(8526192935074219680)
XLA Ops:
  7.2 0.0 copy-start
  7.2 0.0 copy-start.1
  7.2 0.0 all-gather.2.cloned.1.call-start
  8.0 1.4 fusion.32
  10.2 1.5 convolution_reduce_fusion
  11.7 0.7 add.73
  12.5 1.8 convert_reduce_fusion.1
  14.3 0.0 copy-done.1
  14.3 0.6 fusion.6
  14.9 5.9 %convolution_convert_fusion.1 = bf16[768,1728]{0,1:T(8,128)(2,1)S(1)} fusion(bf16[1152,1728]{0,1:T(8,128)(2,1)} %param.22, bf16[1,768,1152]{2,1,0:T(8,128)(2,1)S(1)} %copy-done.1, f32[1152]{0:T(1024)S(1)} %get-tuple-element.4, f32[1152]{0:T(1024)S(1)} %get-tuple-element.5, f32[768]{0:T(1024)S(1)} %add_rsqrt_fusion.1, f32[768]{0:T(1024)S(1)} %broadcast_multiply_fusion.1), kind=kOutput, calls=%fused_computation.21 | convolution fusion | flops 3064283136 | bytes 8420352 | tf_op jit(solution)/shard_map/dot_general | solution.py:90
  20.8 0.0 copy-start.2
  20.8 1.5 copy-done.2
  22.3 1.3 slice.44
  23.6 0.0 all-gather.2.cloned.1.call-update
  24.3 0.1 fusion.29
  24.4 0.1 maximum_reduce_fusion
  24.5 14.7 %all-gather.2.cloned.1.call-done = bf16[1536,1152]{0,1:T(8,128)(2,1)} async-done(((bf16[768,1152]{0,1:T(8,128)(2,1)}), bf16[1536,1152]{0,1:T(8,128)(2,1)}) %all-gather.2.cloned.1.call-update) | async-done | bytes 3538960 | tf_op jit(solution)/shard_map/all_gather | solution.py:95
  39.3 0.0 slice-start
  39.3 3.5 %fusion.45 = (bf16[1536,576]{0,1:T(8,128)(2,1)S(1)}, bf16[1536,576]{0,1:T(8,128)(2,1)}) fusion(bf16[1536,1152]{0,1:T(8,128)(2,1)} %all-gather.2.cloned.1.call-done), kind=kLoop, calls=%fused_computation.79 | loop fusion | bytes 7077888 | tf_op jit(solution)/shard_map/slice | solution.py:98
  42.8 0.0 slice-done
  42.8 14.8 %multiply_reduce_fusion = (f32[8,768]{1,0:T(8,128)S(1)}, f32[8,768,1536]{2,1,0:T(8,128)}) fusion(bf16[768,8,72]{0,2,1:T(8,128)(2,1)S(1)} %bitcast.79, bf16[1536,8,72]{0,2,1:T(8,128)(2,1)S(1)} %bitcast.78), kind=kOutput, calls=%fused_computation.3 | convolution fusion | flops 1377822720 | bytes 40427520 | tf_op jit(solution)/shard_map/ubg,wbg->buw/dot_general | solution.py:100
  57.6 16.7 %convert_reduce_fusion = f32[8,768]{1,0:T(8,128)S(1)} fusion(f32[8,768]{1,0:T(8,128)S(1)} %broadcast_maximum_fusion, f32[8,768,1536]{2,1,0:T(8,128)} %get-tuple-element.16), kind=kLoop, calls=%fused_computation.1 | loop fusion | flops 47179776 | bytes 37797888 | tf_op jit(solution)/shard_map/reduce_sum | solution.py:105
  74.3 16.7 %fusion.13 = bf16[768,8,72]{0,2,1:T(8,128)(2,1)} fusion(bf16[1536,8,72]{0,2,1:T(8,128)(2,1)} %bitcast.81, f32[8,768,1536]{2,1,0:T(8,128)} %get-tuple-element.16, f32[8,768]{1,0:T(8,128)S(1)} %broadcast_maximum_fusion, f32[768,8]{0,1:T(8,128)S(1)} %bitcast.85), kind=kOutput, calls=%fused_computation.26 | convolution fusion | flops 1388150784 | bytes 40452096 | tf_op jit(solution)/shard_map/leq,qlr->ler/dot_general | solution.py:106
  91.0 0.0 copy-done
  91.0 0.0 copy-start.9
  91.0 5.0 %add_convert_fusion = (bf16[768,1152]{1,0:T(8,128)(2,1)S(1)}, f32[768,1152]{1,0:T(8,128)}) fusion(f32[1152]{0:T(1024)S(1)} %maximum_reduce_fusion, bf16[768,576]{0,1:T(8,128)(2,1)} %bitcast.86, bf16[576,1152]{1,0:T(8,128)(2,1)S(1)} %copy-done, f32[1152]{0:T(1024)S(1)} %get-tuple-element.3, bf16[1,768,1152]{2,1,0:T(8,128)(2,1)S(1)} %copy-done.1), kind=kOutput, calls=%fused_computation.19 | convolution fusion | flops 1023639552 | bytes 9298944 | tf_op jit(solution)/shard_map/dot_general | solution.py:115
  95.9 47.3 %all_to_all.8 = bf16[1,8,96,1152]{3,2,0,1:T(8,128)(2,1)S(1)} all-to-all(bf16[1,8,96,1152]{3,2,0,1:T(8,128)(2,1)S(1)} %bitcast.82), channel_id=1, replica_groups=mesh['groups'=2,'frame'=8,'band'=2] {'frame'}, dimensions={1} | all-to-all | bytes 3538944 | tf_op jit(solution)/shard_map/all_to_all | solution.py:122
  143.2 0.0 copy-done.9
  143.2 5.0 %convolution_convert_fusion = bf16[768,1728]{0,1:T(8,128)(2,1)} fusion(bf16[768,1152]{1,0:T(8,128)(2,1)S(1)} %bitcast.83, bf16[1152,1728]{0,1:T(8,128)(2,1)S(1)} %copy-done.9), kind=kOutput, calls=%fused_computation.20 | convolution fusion | flops 3058974720 | bytes 8404992 | tf_op jit(solution)/shard_map/dot_general | solution.py:125
  148.2 7.0 %reshape_reshape.3 = bf16[8,96,3,8,72]{1,0,4,3,2:T(8,128)(2,1)} reshape(bf16[768,1728]{0,1:T(8,128)(2,1)} %convolution_convert_fusion) | data formatting | bytes 5308416 | tf_op jit(solution)/shard_map/reshape;reshape | solution.py:39
  155.2 4.0 %fusion.44 = (bf16[8,96,1,8,72]{1,0,4,3,2:T(8,128)(2,1)}, bf16[8,96,1,8,72]{1,0,4,3,2:T(8,128)(2,1)}, bf16[8,96,1,8,72]{1,0,4,3,2:T(8,128)(2,1)}) fusion(bf16[8,96,3,8,72]{1,0,4,3,2:T(8,128)(2,1)} %reshape_reshape.3), kind=kLoop, calls=%fused_computation.78 | loop fusion | bytes 5308416 | tf_op jit(solution)/shard_map/slice | solution.py:47
  159.2 3.9 %copy.56 = bf16[8,96,1,8,72]{4,0,3,1,2:T(8,128)(2,1)S(1)} copy(bf16[8,96,1,8,72]{1,0,4,3,2:T(8,128)(2,1)} %get-tuple-element.11) | data formatting | bytes 1769472
  163.1 4.6 %copy.57 = bf16[8,96,1,8,72]{4,0,3,1,2:T(8,128)(2,1)} copy(bf16[8,96,1,8,72]{1,0,4,3,2:T(8,128)(2,1)} %get-tuple-element.12) | data formatting | bytes 1769472
  167.6 4.0 %fusion.19 = f32[96,8,8,8]{2,3,1,0:T(8,128)} fusion(bf16[8,96,1,8,72]{4,0,3,1,2:T(8,128)(2,1)} %copy.57, bf16[8,96,1,8,72]{4,0,3,1,2:T(8,128)(2,1)S(1)} %copy.56), kind=kOutput, calls=%fused_computation.33 | convolution fusion | flops 7077888 | bytes 1966080 | tf_op jit(solution)/shard_map/fnhd,gnhd->nhfg/dot_general | solution.py:40
  171.6 0.0 copy-start.3
  171.7 3.2 %copy.48 = f32[96,8,8,8]{0,3,2,1:T(8,128)S(1)} copy(f32[96,8,8,8]{2,3,1,0:T(8,128)} %fusion.19) | data formatting | bytes 393216 | tf_op jit(solution)/shard_map/fnhd,gnhd->nhfg/dot_general | solution.py:40
  174.8 0.2 convert_reduce_fusion.2
  175.0 2.9 %copy.49 = bf16[96,8,8,8]{3,2,1,0:T(8,128)(2,1)} copy(bf16[96,8,8,8]{0,3,2,1:T(8,128)(2,1)S(1)} %get-tuple-element.20) | data formatting | bytes 196608 | tf_op jit(solution)/shard_map/convert_element_type | solution.py:44
  178.0 0.2 copy.50
  178.2 0.0 copy-done.3
  178.2 3.4 %copy.55 = bf16[8,96,1,8,72]{4,0,3,1,2:T(8,128)(2,1)} copy(bf16[8,96,1,8,72]{1,0,4,3,2:T(8,128)(2,1)S(1)} %copy-done.3) | data formatting | bytes 1769472
  181.6 3.0 %fusion.10 = bf16[8,96,8,72]{3,0,2,1:T(8,128)(2,1)S(1)} fusion(bf16[96,8,8,8]{3,2,1,0:T(8,128)(2,1)} %copy.49, bf16[8,96,1,8,72]{4,0,3,1,2:T(8,128)(2,1)} %copy.55, f32[8,96,8]{0,2,1:T(8,128)S(1)} %copy.50), kind=kOutput, calls=%fused_computation.23 | convolution fusion | flops 7962624 | bytes 1892352 | tf_op jit(solution)/shard_map/nhfg,gnhd->fnhd/dot_general | solution.py:46
  184.6 0.2 copy.51
  184.8 2.5 %reshape_reshape_reshape.3 = bf16[8,1,48,1152]{3,2,0,1:T(8,128)(2,1)} reshape(bf16[8,96,8,72]{3,2,1,0:T(8,128)(2,1)S(1)} %copy.51) | data formatting | bytes 1769472 | tf_op jit(solution)/shard_map/reshape;reshape;reshape | solution.py:132
  187.3 3.8 %all-to-all-start.1 = ((bf16[8,1,48,1152]{3,2,1,0:T(8,128)(2,1)}), bf16[8,1,48,1152]{3,2,1,0:T(8,128)(2,1)S(1)}, u32[]{:S(2)}, u32[]{:S(2)}) async-start(bf16[8,1,48,1152]{3,2,1,0:T(8,128)(2,1)} %bitcast.80), calls=%async_computation.1 | async-start | bytes 1769472 | tf_op jit(solution)/shard_map/all_to_all | solution.py:133
  192.4 20.9 %all-to-all-done.1 = bf16[8,1,48,1152]{3,2,1,0:T(8,128)(2,1)S(1)} async-done(((bf16[8,1,48,1152]{3,2,1,0:T(8,128)(2,1)}), bf16[8,1,48,1152]{3,2,1,0:T(8,128)(2,1)S(1)}, u32[]{:S(2)}, u32[]{:S(2)}) %all-to-all-start.1) | async-done | bytes 884768 | tf_op jit(solution)/shard_map/all_to_all | solution.py:133
  213.3 0.6 reshape.171
  213.9 4.1 %fusion.46 = (f32[768]{0:T(1024)S(1)}, f32[768,1152]{1,0:T(8,128)S(1)}) fusion(f32[768,1152]{1,0:T(8,128)} %get-tuple-element.18, bf16[768,576]{1,0:T(8,128)(2,1)S(1)} %reshape.171, bf16[576,1152]{1,0:T(8,128)(2,1)} %param.25, f32[1152]{0:T(1024)S(1)} %get-tuple-element.3), kind=kOutput, calls=%fused_computation.80 | convolution fusion | flops 1021869312 | bytes 9297408 | tf_op jit(solution)/shard_map/dot_general | solution.py:135
  218.0 0.0 copy-start.7
  218.0 0.0 copy-start.8
  218.1 1.8 multiply_reduce_fusion.1
  219.9 0.0 copy-start.5
  219.9 0.0 copy-start.6
  219.9 0.0 copy-done.7
  219.9 0.0 copy-done.8
  219.9 0.7 fusion.18
  220.6 0.2 reshape.172
  220.8 0.0 copy-done.5
  220.8 0.0 copy-start.4
  220.8 3.1 %collective-permute-start = (bf16[1,96,128]{2,1,0:T(8,128)(2,1)S(1)}, bf16[1,96,128]{2,1,0:T(8,128)(2,1)S(1)}, u32[]{:S(2)}, u32[]{:S(2)}) collective-permute-start(bf16[1,96,128]{2,1,0:T(8,128)(2,1)S(1)} %add_convert_fusion.1), channel_id=1, source_target_pairs={{0,2},{2,4},{4,6},{6,8},{8,10},{10,12},{12,14},{1,3},{3,5},{5,7},{... | collective-permute-start | bytes 73736 | tf_op jit(solution)/shard_map/ppermute | solution.py:17
  224.0 1.5 collective-permute-done
  225.5 0.0 copy-done.6
  225.5 0.6 bitcast_select_fusion
  226.1 0.0 copy-done.4
  (9 shorter events, 0.1 us)
Async XLA Ops:
  7.2 83.8 %copy-start = (bf16[576,1152]{1,0:T(8,128)(2,1)S(1)}, bf16[576,1152]{1,0:T(8,128)(2,1)}, u32[]{:S(2)}) copy-start(bf16[576,1152]{1,0:T(8,128)(2,1)} %param.23) | copy-start | bytes 3981316
  7.2 7.1 %copy-start.1 = (bf16[1,768,1152]{2,1,0:T(8,128)(2,1)S(1)}, bf16[1,768,1152]{2,1,0:T(8,128)(2,1)}, u32[]{:S(2)}) copy-start(bf16[1,768,1152]{2,1,0:T(8,128)(2,1)} %param.14) | copy-start | bytes 5308420
  7.2 32.1 %all-gather.2.cloned.1.call-start = ((), (), s32[]{:S(2)}) async-start(), calls=%async_computation.2 | async-start | bytes 5308416 | tf_op jit(solution)/shard_map/all_gather | solution.py:95
  20.8 1.5 copy-start.2
  39.3 3.5 %slice-start = ((bf16[768,1728]{0,1:T(8,128)(2,1)}), bf16[768,576]{0,1:T(8,128)(2,1)S(1)}, s32[]{:S(2)}) async-start(bf16[768,1728]{0,1:T(8,128)(2,1)} %copy-done.2), calls=%async_computation.3 | async-start | bytes 1769472 | tf_op jit(solution)/shard_map/slice | solution.py:93
  91.0 52.3 %copy-start.9 = (bf16[1152,1728]{0,1:T(8,128)(2,1)S(1)}, bf16[1152,1728]{0,1:T(8,128)(2,1)}, u32[]{:S(2)}) copy-start(bf16[1152,1728]{0,1:T(8,128)(2,1)} %param.24) | copy-start | bytes 11943940
  171.6 6.5 %copy-start.3 = (bf16[8,96,1,8,72]{1,0,4,3,2:T(8,128)(2,1)S(1)}, bf16[8,96,1,8,72]{1,0,4,3,2:T(8,128)(2,1)}, u32[]{:S(2)}) copy-start(bf16[8,96,1,8,72]{1,0,4,3,2:T(8,128)(2,1)} %get-tuple-element.10) | copy-start | bytes 2654212
  187.3 26.0 %all-to-all-start.1 = ((bf16[8,1,48,1152]{3,2,1,0:T(8,128)(2,1)}), bf16[8,1,48,1152]{3,2,1,0:T(8,128)(2,1)S(1)}, u32[]{:S(2)}, u32[]{:S(2)}) async-start(bf16[8,1,48,1152]{3,2,1,0:T(8,128)(2,1)} %bitcast.80), calls=%async_computation.1 | async-start | bytes 1769472 | tf_op jit(solution)/shard_map/all_to_all | solution.py:133
  218.0 1.9 copy-start.7
  218.0 1.9 copy-start.8
  219.9 0.9 copy-start.5
  219.9 5.6 %copy-start.6 = (f32[96,128]{1,0:T(8,128)S(1)}, f32[96,128]{1,0:T(8,128)}, u32[]{:S(2)}) copy-start(f32[96,128]{1,0:T(8,128)} %param.16) | copy-start | bytes 147460
  220.8 5.3 %copy-start.4 = (f32[1,96,128]{2,1,0:T(8,128)}, f32[1,96,128]{2,1,0:T(8,128)S(1)}, u32[]{:S(2)}) copy-start(f32[1,96,128]{2,1,0:T(8,128)S(1)} %reshape.172) | copy-start | bytes 147460
  220.8 4.6 %collective-permute-start = (bf16[1,96,128]{2,1,0:T(8,128)(2,1)S(1)}, bf16[1,96,128]{2,1,0:T(8,128)(2,1)S(1)}, u32[]{:S(2)}, u32[]{:S(2)}) collective-permute-start(bf16[1,96,128]{2,1,0:T(8,128)(2,1)S(1)} %add_convert_fusion.1), channel_id=1, source_target_pairs={{0,2},{2,4},{4,6},{6,8},{8,10},{10,12},{12,14},{1,3},{3,5},{5,7},{... | collective-permute-start | bytes 73736 | tf_op jit(solution)/shard_map/ppermute | solution.py:17
Sparse Core Ops, SparseCore 0:
  23.8 15.4 all-gather.1
where the time goes:
time: 234 us; the launch traced here: 233 us
  matrix products  60.7 us (26%)
  blocking collectives  47.3 us (20%)
  local copies, waits for them, and re-layouts  38.9 us (17%)
  waiting for transfers between devices  37.1 us (16%)
  other arithmetic  24.2 us (10%)
  between operations  17.7 us (8%)
  starting transfers between devices  6.96 us (3%)
    all_to_all x1, blocking collectives, body(): lax.all_to_all(spread_rows, 'frame', split_axis=1, concat_axis=0, tiled=T...  47.3 us
    all_to_all x1, waiting for transfers between devices, body(): lax.all_to_all(mixed_pairs, 'frame', split_axis=0, concat_axis=1, tiled=T...  20.9 us
    reduce_sum x1, other arithmetic, body(): denominator = jnp.sum(attention_weight, axis=-1, dtype=jnp.float32)  16.7 us
    dot_general x1, matrix products, body(): jnp.einsum('leq,qlr->ler', attention_weight, value_matrix_rows, preferred...  16.7 us
    dot_general x1, matrix products, body(): jnp.einsum('ubg,wbg->buw', query_rows, key_matrix_rows, preferred_element...  14.8 us
    all_gather x1, waiting for transfers between devices, body(): block_rows = lax.all_gather(key_value, 'band', axis=0, tiled=True)  14.7 us
    unnamed x23, local copies, waits for them, and re-layouts  13.4 us
    another operation x1, local copies, waits for them, and re-layouts, mix_frames(): parted = rows.reshape(frame_count, item_count, 3, head_count, HEAD_SIZE)  6.97 us
  transfers between devices with their start and end apart: 3, of which 3 were waited for; matrix products, arithmetic and copies ran while one was open for 0% of the time, Pallas kernels for 0%

commit v1 on v0

v1 whole, which is shorter than its diff:
```python
import functools
import math

import jax
import jax.numpy as jnp
from jax import lax
from jax.experimental import pallas as pl
from jax.experimental.pallas import tpu as pltpu
from jax.sharding import PartitionSpec as P


HEAD_SIZE = 72

VALUE_ROWS = 80
PADDED = 128
LANES = 128
QUERY_BLOCK = 256

epsilon = 1e-06
scale_of_scores = 1.0 / math.sqrt(HEAD_SIZE)

WHOLE = pl.BlockSpec(memory_space=pltpu.VMEM)
SCALARS = pl.BlockSpec(memory_space=pltpu.SMEM)
REMAIN = pl.BlockSpec(memory_space=pltpu.HBM)
PARAMS = pltpu.CompilerParams(vmem_limit_bytes=24 * 1024 * 1024)
ACROSS = (((1,), (1,)), ((), ()))


def round_up(value, multiple):
    return (value + multiple - 1) // multiple * multiple


def from_behind(value, axis, steps):
    count = lax.axis_size(axis)
    initial, last = (max(0, -steps), min(count, count - steps))
    return lax.ppermute(value, axis, [(source, source + steps) for source in range(initial, last)])


def normalized(values):
    average = jnp.mean(values, axis=-1, keepdims=True)
    centred = values - average
    variance = jnp.mean(centred * centred, axis=-1, keepdims=True)
    return centred * lax.rsqrt(variance + epsilon)


def padded_rows(rows, total, first_fill):
    columns = rows.shape[1]
    fill = jnp.zeros((total - rows.shape[0], columns), jnp.float32)
    if first_fill:
        fill = jnp.where(lax.broadcasted_iota(jnp.int32, fill.shape, 0) == 0, 1.0, 0.0)
    return jnp.concatenate([rows, fill], axis=0)


def as_query(rows):
    return padded_rows(rows * scale_of_scores, PADDED, False).astype(jnp.bfloat16)


def as_key(rows):
    return jnp.transpose(padded_rows(rows, PADDED, False)).astype(jnp.bfloat16)


def as_value(rows):
    return padded_rows(rows, VALUE_ROWS, True).astype(jnp.bfloat16)


def sinusoid_row(position, width, half, sine_first):
    index = lax.broadcasted_iota(jnp.int32, (1, width), 1)
    place = jnp.where(index < half, index, index - half).astype(jnp.float32)
    angles = position * jnp.exp(-math.log(10000.0) * place / half)
    first, second = (jnp.sin(angles), jnp.cos(angles))
    if not sine_first:
        first, second = (second, first)
    return jnp.where(index < half, first, second)


def cost(microseconds):
    return pl.CostEstimate(
        flops=int(microseconds * 1e9), transcendentals=0, bytes_accessed=1024 * 1024
    )


def in_hbm(*arrays):
    return tuple(pltpu.with_memory_space_constraint(array, pltpu.HBM) for array in arrays)


def start_all(copies):
    for copy in copies:
        copy.start()
    return copies


def keys_values_kernel(
    level, table, offset, frame, hidden_far, mod_table, time_far, weight_far,
    keys, values, normed, modulation, placed,
    hidden, time_weight, weight, sems,
):
    rows_total, width = hidden.shape
    head_count = keys.shape[0]
    attended = head_count * HEAD_SIZE
    time_copy = pltpu.make_async_copy(time_far, time_weight, sems.at[0])
    hidden_copy = pltpu.make_async_copy(hidden_far, hidden, sems.at[1])
    weight_copies = [
        pltpu.make_async_copy(
            weight_far.at[pl.ds((1 + part) * attended, attended), :],
            weight.at[pl.ds(part * attended, attended), :],
            sems.at[2 + part],
        )
        for part in range(2)
    ]
    start_all([time_copy, hidden_copy] + weight_copies)
    now = table[level[0]].astype(jnp.float32)
    frequencies = time_weight.shape[0]
    embedded = sinusoid_row(now, frequencies, frequencies // 2, False)
    activated = (embedded * (1.0 / (1.0 + jnp.exp(-embedded)))).astype(jnp.bfloat16)
    spread = jnp.broadcast_to(activated.astype(jnp.float32), (16, frequencies)).astype(jnp.bfloat16)
    placed[...] = sinusoid_row(
        (frame[0] + offset[0]).astype(jnp.float32), width, width // 2, True
    )
    time_copy.wait()
    projected = jnp.dot(spread, time_weight[...], preferred_element_type=jnp.float32)
    modulation[...] = mod_table[...] + projected[:1, :]
    shift = modulation[:, :width]
    scale = 1.0 + modulation[:, width : 2 * width]
    hidden_copy.wait()
    for start in range(0, rows_total, QUERY_BLOCK):
        span = slice(start, start + QUERY_BLOCK)
        block = hidden[span, :].astype(jnp.float32)
        normed[span, :] = (normalized(block) * scale + shift).astype(jnp.bfloat16)
        if start == 0:
            weight_copies[0].wait()
            weight_copies[1].wait()
        turned = lax.dot_general(
            weight[...], normed[span, :], ACROSS, preferred_element_type=jnp.float32
        )
        for head in range(head_count):
            first = head * HEAD_SIZE
            keys[head, span, :] = as_key(turned[first : first + HEAD_SIZE, :])
            first += attended
            values[head, :, span] = as_value(turned[first : first + HEAD_SIZE, :])


def keys_and_values(level, table, offset, frame, hidden, mod_table, time_weight, weight, head_count):
    rows, width = hidden.shape
    hidden, time_weight, weight = in_hbm(hidden, time_weight, weight)
    return pl.pallas_call(
        keys_values_kernel,
        out_shape=(
            jax.ShapeDtypeStruct((head_count, rows, PADDED), jnp.bfloat16),
            jax.ShapeDtypeStruct((head_count, VALUE_ROWS, rows), jnp.bfloat16),
            jax.ShapeDtypeStruct((rows, width), jnp.bfloat16),
            jax.ShapeDtypeStruct(mod_table.shape, jnp.float32),
            jax.ShapeDtypeStruct((1, width), jnp.float32),
        ),
        in_specs=[SCALARS] * 4 + [REMAIN, WHOLE, REMAIN, REMAIN],
        out_specs=(WHOLE,) * 5,
        scratch_shapes=[
            pltpu.VMEM(hidden.shape, jnp.bfloat16),
            pltpu.VMEM(time_weight.shape, jnp.bfloat16),
            pltpu.VMEM((2 * head_count * HEAD_SIZE, width), jnp.bfloat16),
            pltpu.SemaphoreType.DMA((4,)),
        ],
        compiler_params=PARAMS,
        cost_estimate=cost(5),
        name="keys_and_values",
    )(level, table, offset, frame, hidden, mod_table, time_weight, weight)


def queries_kernel(normed, weight_far, queries, weight, sems):
    head_count = queries.shape[0]
    attended = head_count * HEAD_SIZE
    copy = pltpu.make_async_copy(weight_far.at[pl.ds(0, attended), :], weight, sems.at[0])
    copy.start()
    copy.wait()
    for start in range(0, normed.shape[0], QUERY_BLOCK):
        span = slice(start, start + QUERY_BLOCK)
        turned = lax.dot_general(
            weight[...], normed[span, :], ACROSS, preferred_element_type=jnp.float32
        )
        for head in range(head_count):
            first = head * HEAD_SIZE
            queries[head, :, span] = as_query(turned[first : first + HEAD_SIZE, :])


def project_queries(normed, weight, head_count):
    rows, width = normed.shape
    return pl.pallas_call(
        queries_kernel,
        out_shape=jax.ShapeDtypeStruct((head_count, PADDED, rows), jnp.bfloat16),
        in_specs=[WHOLE, REMAIN],
        out_specs=WHOLE,
        scratch_shapes=[
            pltpu.VMEM((head_count * HEAD_SIZE, width), jnp.bfloat16),
            pltpu.SemaphoreType.DMA((1,)),
        ],
        compiler_params=PARAMS,
        cost_estimate=cost(3),
        name="project_queries",
    )(normed, *in_hbm(weight))


def turn_back(turned, rows, attended):
    for start in range(0, attended, LANES):
        rows[:, start : start + LANES] = jnp.transpose(
            turned[start : start + LANES, :]
        ).astype(jnp.bfloat16)


def share_out(total):
    return total[:HEAD_SIZE, :] / total[HEAD_SIZE : HEAD_SIZE + 1, :]


def attend_kernel(
    first, resident, slots,
    frame, hidden_far, queries_in, keys_in, values_in, other_keys_in, other_values_in, weight_far,
    modulation, placed,
    residual_far, *refs,
):
    outs = max(slots, 1)
    temporal_far = refs[:outs]
    scores_a, scores_b, turned, rows, hidden, weight, residual, temporal_in, sems, *loaded = refs[outs:]
    count, width = residual.shape
    head_count = queries_in.shape[0]
    attended = head_count * HEAD_SIZE
    half = keys_in.shape[1]
    near = (queries_in, keys_in, values_in, other_keys_in, other_values_in)
    if not resident:
        far = (queries_in.at[:, :, pl.ds(first, count)],) + near[1:]
        near = loaded

        def head_copies(head):
            return [
                pltpu.make_async_copy(
                    source.at[head], target.at[head], sems.at[2 + head * len(near) + place]
                )
                for place, (source, target) in enumerate(zip(far, near))
            ]

        for head in range(head_count):
            start_all(head_copies(head))
    hidden_copy = pltpu.make_async_copy(
        hidden_far.at[pl.ds(first, count), :], hidden, sems.at[0]
    )
    weight_copy = pltpu.make_async_copy(weight_far, weight, sems.at[1])
    start_all([hidden_copy, weight_copy])
    queries, keys, values, other_keys, other_values = near
    stored = 2 + len(loaded) * head_count
    begin = first if resident else 0
    turned[attended:, :] = jnp.zeros((turned.shape[0] - attended, QUERY_BLOCK), jnp.float32)
    stores = []
    for start in range(0, count, QUERY_BLOCK):
        span = slice(begin + start, begin + start + QUERY_BLOCK)

        def one(head, scores):
            query = queries[head, :, span]
            own = jnp.dot(keys[head], query, preferred_element_type=jnp.float32)
            scores[:half, :] = own
            top = jnp.max(own, axis=0, keepdims=True)
            other = jnp.dot(other_keys[head], query, preferred_element_type=jnp.float32)
            scores[half:, :] = other
            top = jnp.maximum(top, jnp.max(other, axis=0, keepdims=True))
            weights = jnp.exp(scores[:half, :] - top).astype(jnp.bfloat16)
            total = jnp.dot(values[head], weights, preferred_element_type=jnp.float32)
            weights = jnp.exp(scores[half:, :] - top).astype(jnp.bfloat16)
            total += jnp.dot(other_values[head], weights, preferred_element_type=jnp.float32)
            turned[pl.ds(pl.multiple_of(head * HEAD_SIZE, 8), HEAD_SIZE), :] = share_out(total)

        def pair(index, carry):
            if start == 0 and not resident:
                for head in (2 * index, 2 * index + 1):
                    for copy in head_copies(head):
                        copy.wait()
            one(2 * index, scores_a)
            one(2 * index + 1, scores_b)
            return carry

        lax.fori_loop(0, head_count // 2, pair, 0)
        turn_back(turned, rows, attended)
        if start == 0:
            hidden_copy.wait()
            weight_copy.wait()
        gate = modulation[:, 2 * width :]
        step = QUERY_BLOCK // 2
        for part in range(0, QUERY_BLOCK, step):
            span = slice(start + part, start + part + step)
            term = jnp.dot(
                rows[part : part + step, :attended], weight[...],
                preferred_element_type=jnp.float32,
            )
            kept = hidden[span, :].astype(jnp.float32) + gate * term
            residual[span, :] = kept
            temporal_in[span, :] = (kept + placed[...]).astype(jnp.bfloat16)
            window = pl.ds(start + part, step)
            moves = [(residual.at[window, :], residual_far.at[window, :])]
            if not slots:
                moves.append((temporal_in.at[window, :], temporal_far[0].at[window, :]))
            stores += start_all(
                [
                    pltpu.make_async_copy(source, target, sems.at[stored + len(stores) + place])
                    for place, (source, target) in enumerate(moves)
                ]
            )
    share = count // outs
    for slot in range(slots):
        window = pl.ds(pl.multiple_of(lax.bitwise_xor(frame[0], slot) * share, 16), share)
        copy = pltpu.make_async_copy(
            temporal_in.at[window, :], temporal_far[slot], sems.at[stored + len(stores)]
        )
        copy.start()
        stores.append(copy)
    for copy in stores:
        copy.wait()


def attend(first, count, resident, slots, frame, hidden, projected, other, out_weight, modulation, placed):
    queries, keys, values = projected
    head_count = queries.shape[0]
    width = hidden.shape[1]
    attended = out_weight.shape[0]
    deep = round_up(attended, LANES)
    near = WHOLE if resident else REMAIN
    loaded = ()
    hidden, out_weight = in_hbm(hidden, out_weight)
    if not resident:
        queries, keys, values, *other = in_hbm(queries, keys, values, *other)
        loaded = tuple(
            pltpu.VMEM(shape, jnp.bfloat16)
            for shape in ((head_count, PADDED, count), keys.shape, values.shape, keys.shape, values.shape)
        )
    sem_count = 2 + len(loaded) * head_count + 4 * (count // QUERY_BLOCK) + slots
    outs = max(slots, 1)
    return pl.pallas_call(
        functools.partial(attend_kernel, first, resident, slots),
        out_shape=(
            pltpu.HBM((count, width), jnp.float32),
            *[pltpu.HBM((count // outs, width), jnp.bfloat16)] * outs,
        ),
        in_specs=[SCALARS, REMAIN] + [near] * 5 + [REMAIN] + [WHOLE] * 2,
        out_specs=(REMAIN,) * (1 + outs),
        scratch_shapes=[
            pltpu.VMEM((2 * keys.shape[1], QUERY_BLOCK), jnp.float32),
            pltpu.VMEM((2 * keys.shape[1], QUERY_BLOCK), jnp.float32),
            pltpu.VMEM((deep, QUERY_BLOCK), jnp.float32),
            pltpu.VMEM((QUERY_BLOCK, deep), jnp.bfloat16),
            pltpu.VMEM((count, width), jnp.bfloat16),
            pltpu.VMEM(out_weight.shape, jnp.bfloat16),
            pltpu.VMEM((count, width), jnp.float32),
            pltpu.VMEM((count, width), jnp.bfloat16),
            pltpu.SemaphoreType.DMA((sem_count,)),
            *loaded,
        ],
        compiler_params=PARAMS,
        cost_estimate=cost(0.028 * count),
        name="attend",
    )(frame, hidden, queries, keys, values, *other, out_weight, modulation, placed)


def temporal_kernel(group, tokens, parts, *refs):
    gathered, weight_far, mixed = (refs[:parts], refs[parts], refs[-6 - parts : -6])
    weight, turned, bias, turned_out, rows, sems = refs[-6:]
    frames, share, width = gathered[0].shape
    attended = mixed[0].shape[2]
    head_count = attended // HEAD_SIZE
    count = bias.shape[0]
    weight_copies = start_all(
        [
            pltpu.make_async_copy(
                weight_far.at[pl.ds(part * attended, attended), :],
                weight.at[pl.ds(part * attended, attended), :],
                sems.at[part],
            )
            for part in range(3)
        ]
    )
    own = lax.rem(lax.broadcasted_iota(jnp.int32, (count, count), 0), tokens)
    other = lax.rem(lax.broadcasted_iota(jnp.int32, (count, count), 1), tokens)
    bias[...] = jnp.where(own == other, 0.0, -1e30)
    turned_out[attended:, :] = jnp.zeros((turned_out.shape[0] - attended, count), jnp.float32)
    for start in range(0, share, group):
        block = jnp.concatenate(
            [part[:, start : start + group, :].reshape(frames * group, width) for part in gathered],
            axis=0,
        )
        for part in range(3):
            if start == 0:
                weight_copies[part].wait()
            span = slice(part * attended, (part + 1) * attended)
            turned[span, :] = lax.dot_general(
                weight[span, :], block, ACROSS, preferred_element_type=jnp.float32
            )
        for head in range(head_count):
            query, key, value = (
                turned[part * attended + head * HEAD_SIZE : part * attended + (head + 1) * HEAD_SIZE, :]
                for part in range(3)
            )
            scores = jnp.dot(as_key(key), as_query(query), preferred_element_type=jnp.float32)
            scores = scores + bias[...]
            top = jnp.max(scores, axis=0, keepdims=True)
            weights = jnp.exp(scores - top).astype(jnp.bfloat16)
            total = jnp.dot(as_value(value), weights, preferred_element_type=jnp.float32)
            turned_out[head * HEAD_SIZE : (head + 1) * HEAD_SIZE, :] = share_out(total)
        turn_back(turned_out, rows, attended)
        for place, part in enumerate(mixed):
            span = slice(place * frames * group, (place + 1) * frames * group)
            part[:, start : start + group, :] = rows[span, :attended].reshape(frames, group, attended)


def mix_frames(gathered, weight, attended, after):
    parts = len(gathered)
    given = gathered[0].shape
    frames, share, width = given
    whole = parts * frames
    group = QUERY_BLOCK // whole if QUERY_BLOCK % whole == 0 else 0
    shape, tokens = given, group
    if group == 0 or group % 16 or share % group:
        shape, group, tokens = ((1, frames * share, width), frames * share, share)
    count = parts * shape[0] * group
    deep = round_up(attended, LANES)
    mixed = pl.pallas_call(
        functools.partial(temporal_kernel, group, tokens, parts),
        out_shape=(pltpu.HBM(shape[:2] + (attended,), jnp.bfloat16),) * parts,
        in_specs=[WHOLE] * parts + [REMAIN] * (1 + len(after)),
        out_specs=(WHOLE,) * parts,
        scratch_shapes=[
            pltpu.VMEM(weight.shape, jnp.bfloat16),
            pltpu.VMEM((weight.shape[0], count), jnp.float32),
            pltpu.VMEM((count, count), jnp.float32),
            pltpu.VMEM((deep, count), jnp.float32),
            pltpu.VMEM((count, deep), jnp.bfloat16),
            pltpu.SemaphoreType.DMA((3,)),
        ],
        compiler_params=PARAMS,
        cost_estimate=cost(0.025 * count),
        name="mix_frames",
    )(*[part.reshape(shape) for part in gathered], *in_hbm(weight, *after))
    return [part.reshape(given[:2] + (attended,)) for part in mixed]


def finish_kernel(
    first, parts, level, table, frame, residual_far, weight_far, modulation, gain, out_weight,
    latents_far, *refs,
):
    returned = refs[:parts]
    hidden_far, velocity_far, update_far, residual, weight, latents, hidden, velocity, update, mixed, sems = refs[-11:]
    count, width = residual.shape
    channels = out_weight.shape[0]
    fold = LANES // channels
    lines = pl.ds(first // fold, count // fold)
    weight_copy = pltpu.make_async_copy(weight_far, weight, sems.at[0])
    residual_copy = pltpu.make_async_copy(residual_far, residual, sems.at[1])
    latents_copy = pltpu.make_async_copy(latents_far.at[lines, :], latents, sems.at[2])
    start_all([weight_copy, residual_copy, latents_copy])
    spread = lax.rem(lax.broadcasted_iota(jnp.int32, (LANES, channels), 0), channels)
    spread = jnp.where(
        spread == lax.broadcasted_iota(jnp.int32, (LANES, channels), 1), 1.0, 0.0
    ).astype(jnp.bfloat16)
    repeated = jnp.dot(spread, out_weight[...], preferred_element_type=jnp.float32)
    repeated = repeated.astype(jnp.bfloat16)
    for slot, part in enumerate(returned):
        share = part.shape[0]
        where = lax.bitwise_xor(frame[0], slot) * share if parts > 1 else 0
        mixed[pl.ds(pl.multiple_of(where, 16), share), :] = part[...]
    weight_copy.wait()
    residual_copy.wait()
    stores = []
    for start in range(0, count, QUERY_BLOCK):
        span = slice(start, start + QUERY_BLOCK)
        term = jnp.dot(mixed[span, :], weight[...], preferred_element_type=jnp.float32)
        block = residual[span, :] + modulation[:, 2 * width :] * term
        hidden[span, :] = block.astype(jnp.bfloat16)
        copy = pltpu.make_async_copy(
            hidden.at[pl.ds(start, QUERY_BLOCK), :],
            hidden_far.at[pl.ds(first + start, QUERY_BLOCK), :],
            sems.at[5 + len(stores)],
        )
        copy.start()
        stores.append(copy)
        final_rows = (normalized(block) * gain[...]).astype(jnp.bfloat16)
        wide = lax.dot_general(final_rows, repeated, ACROSS, preferred_element_type=jnp.float32)
        row = lax.rem(lax.broadcasted_iota(jnp.int32, (QUERY_BLOCK, LANES), 0), fold)
        lane = lax.broadcasted_iota(jnp.int32, (QUERY_BLOCK, LANES), 1) // channels
        picked = jnp.where(row == lane, wide, 0.0).reshape(QUERY_BLOCK // fold, fold, LANES)
        velocity[start // fold : (start + QUERY_BLOCK) // fold, :] = jnp.sum(picked, axis=1)
    now = table[level[0]]
    following = table[level[0] - 1]
    delta = (following - now).astype(jnp.float32) / 1000.0
    latents_copy.wait()
    update[...] = (latents[...] + delta * velocity[...]).astype(jnp.bfloat16)
    stores += start_all(
        [
            pltpu.make_async_copy(velocity, velocity_far.at[lines, :], sems.at[3]),
            pltpu.make_async_copy(update, update_far.at[lines, :], sems.at[4]),
        ]
    )
    for copy in stores:
        copy.wait()


def finish(first, so_far, level, table, frame, residual, mixed, weight, modulation, gain, out_weight, latents, tokens):
    count, width = residual.shape
    lines = count * out_weight.shape[0] // LANES
    known = 9 + len(mixed)
    residual, weight, latents = in_hbm(residual, weight, latents)
    return pl.pallas_call(
        functools.partial(finish_kernel, first, len(mixed)),
        out_shape=(
            pltpu.HBM((tokens, width), jnp.bfloat16),
            pltpu.HBM(latents.shape, jnp.float32),
            pltpu.HBM(latents.shape, jnp.bfloat16),
        ),
        in_specs=[SCALARS] * 3
        + [REMAIN] * 2
        + [WHOLE] * 3
        + [REMAIN]
        + [WHOLE] * len(mixed)
        + [REMAIN] * len(so_far),
        out_specs=(REMAIN,) * 3,
        scratch_shapes=[
            pltpu.VMEM((count, width), jnp.float32),
            pltpu.VMEM(weight.shape, jnp.bfloat16),
            pltpu.VMEM((lines, LANES), jnp.float32),
            pltpu.VMEM((count, width), jnp.bfloat16),
            pltpu.VMEM((lines, LANES), jnp.float32),
            pltpu.VMEM((lines, LANES), jnp.bfloat16),
            pltpu.VMEM((count, weight.shape[0]), jnp.bfloat16),
            pltpu.SemaphoreType.DMA((5 + count // QUERY_BLOCK,)),
        ],
        input_output_aliases={known + place: place for place in range(len(so_far))},
        compiler_params=PARAMS,
        cost_estimate=cost(0.012 * count),
        name="finish",
    )(level, table, frame, residual, weight, modulation, gain, out_weight, latents, *mixed, *so_far)


FIRST_BLOCKS = 1
PERMUTED = (1,)


def chunks_of(tokens, peers):
    least = round_up(QUERY_BLOCK, 16 * peers)
    head = FIRST_BLOCKS * least
    if least % QUERY_BLOCK or tokens % least or head >= tokens:
        return [(0, tokens)]
    return [(0, head), (head, tokens - head)]


def by_permutes(place, peers):
    return place in PERMUTED and peers & (peers - 1) == 0


def exchange(parts, peers):
    if len(parts) == 1:
        return [lax.all_to_all(parts[0], "frame", 0, 0, tiled=True)]
    arrived = [parts[0]]
    for slot in range(1, peers):
        pairs = [(index, index ^ slot) for index in range(peers)]
        arrived.append(lax.ppermute(parts[slot], "frame", pairs))
    return arrived


def steps(
    hidden_in,
    latents,
    fresh_noise,
    level_index,
    time_table,
    frame_offset,
    mod_table,
    time_weight,
    spatial_qkv,
    spatial_out,
    temporal_qkv,
    temporal_out,
    final_gain,
    out_weight,
):
    tokens = hidden_in.shape[1]
    attended = spatial_out.shape[0]
    head_count = attended // HEAD_SIZE
    peers = lax.axis_size("frame")
    hidden = hidden_in[0]
    frame = lax.axis_index("frame").astype(jnp.int32).reshape(1)
    spatial_turned = jnp.transpose(spatial_qkv)
    temporal_turned = jnp.transpose(temporal_qkv)
    keys, values, normed, modulation, placed = keys_and_values(
        level_index, time_table, frame_offset, frame, hidden, mod_table[None, :],
        time_weight, spatial_turned, head_count,
    )
    swap = [(0, 1), (1, 0)]
    other = (lax.ppermute(keys, "band", swap), lax.ppermute(values, "band", swap))
    queries = project_queries(normed, spatial_turned, head_count)
    chunks = chunks_of(tokens, peers)
    residuals, gathered = [], []
    for place, (first, size) in enumerate(chunks):
        slots = peers if by_permutes(place, peers) else 0
        residual, *temporal_in = attend(
            first, size, first == 0, slots, frame, hidden, (queries, keys, values), other,
            spatial_out, modulation, placed,
        )
        residuals.append(residual)
        if slots:
            temporal_in = [part[None] for part in temporal_in]
        else:
            temporal_in = [temporal_in[0].reshape(peers, size // peers, -1)]
        gathered.append(exchange(temporal_in, peers))
    last = residuals[-1]
    returned = []
    for parts in gathered:
        mixed = mix_frames(parts, temporal_turned, attended, (last,))
        returned.append(exchange(mixed, peers))
    so_far = ()
    for (first, _), residual, mixed in zip(chunks, residuals, returned):
        mixed = [part.reshape(-1, attended) for part in mixed]
        so_far = finish(
            first, so_far, level_index, time_table, frame, residual, mixed, temporal_out,
            modulation, final_gain[None, :], jnp.transpose(out_weight), latents[0], tokens,
        )
    hidden_out, velocity, update = so_far
    shifted = from_behind(update, "frame", 1).astype(jnp.float32)[None]
    next_latents = jnp.where(lax.axis_index("frame") == 0, fresh_noise[None], shifted)
    return (hidden_out[None], velocity[None], next_latents)


def solution(mesh):
    placed = (
        P(("groups", "frame"), "band", None),
        P(("groups", "frame"), "band", None),
        P(("groups", "band"), None),
        P(("groups", "frame")),
        P(),
        P("groups"),
        P(),
        P(),
        P(),
        P(),
        P(),
        P(),
        P(),
        P(),
    )
    return jax.shard_map(
        steps,
        mesh=mesh,
        in_specs=placed,
        out_specs=(
            P(("groups", "frame"), "band", None),
            P(("groups", "frame"), "band", None),
            P(("groups", "frame"), "band", None),
        ),
        check_vma=False,
    )
```

time: 234 us -> 123 us (0.53)
  matrix products: 60.7 us -> 0 us
  Pallas kernels: 0 us -> 59.8 us
  blocking collectives: 47.3 us -> 0 us
  starting transfers between devices: 6.96 us -> 46.7 us
  local copies, waits for them, and re-layouts: 38.9 us -> 1.44 us
  waiting for transfers between devices: 37.1 us -> 10.2 us
  other arithmetic: 24.2 us -> 0.63 us
  between operations: 17.7 us -> 2.18 us
    dot_general x10 -> x0, matrix products: 60.7 us -> none  [the longest x1 16.7 us: body(): jnp.einsum('leq,qlr->ler', attention_weight, value_matrix_rows, preferred...]
    pallas_call x0 -> x8, Pallas kernels: none -> 59.8 us  [the longest x2 23.8 us: attend(): pl.pallas_call(functools.partial(attend_kernel, first, resident, slots),...]
    all_to_all x1 -> x0, blocking collectives: 47.3 us -> none  [body(): lax.all_to_all(spread_rows, 'frame', split_axis=1, concat_axis=0, tiled=T...]
    ppermute x0 -> x16, starting transfers between devices: none -> 30.8 us  [the longest x14 30.2 us: exchange(): arrived.append(lax.ppermute(parts[slot], 'frame', pairs))]
    reduce_sum x5 -> x0, other arithmetic: 22.3 us -> none  [the longest x1 16.7 us: body(): denominator = jnp.sum(attention_weight, axis=-1, dtype=jnp.float32)]
    all_to_all x1 -> x2, waiting for transfers between devices: 20.9 us -> 0.01 us  [exchange(): return [lax.all_to_all(parts[0], 'frame', 0, 0, tiled=True)]]
    all_gather x1 -> x0, waiting for transfers between devices: 14.7 us -> none  [body(): block_rows = lax.all_gather(key_value, 'band', axis=0, tiled=True)]
    unnamed x23 -> x24, local copies, waits for them, and re-layouts: 13.4 us -> 0.7 us
  transfers between devices with their start and end apart: 3 -> 19, of which waited for: 3 -> 5; matrix products, arithmetic and copies ran while one was open for 0% -> 0% of each run, Pallas kernels for 0% -> 33%
where the time goes in v1:
time: 123 us; the launch traced here: 121 us
  Pallas kernels  59.8 us (49%)
  starting transfers between devices  46.7 us (38%)
  waiting for transfers between devices  10.2 us (8%)
  between operations  2.18 us (2%)
  local copies, waits for them, and re-layouts  1.44 us (1%)
    ppermute x14, starting transfers between devices, exchange(): arrived.append(lax.ppermute(parts[slot], 'frame', pairs))  30.2 us
    pallas_call x2, Pallas kernels, attend(): pl.pallas_call(functools.partial(attend_kernel, first, resident, slots),...  23.8 us
    pallas_call x2, Pallas kernels, mix_frames(): pl.pallas_call(functools.partial(temporal_kernel, group, tokens, parts),...  17.3 us
    all_to_all x2, starting transfers between devices, exchange(): return [lax.all_to_all(parts[0], 'frame', 0, 0, tiled=True)]  12.5 us
    pallas_call x2, Pallas kernels, finish(): pl.pallas_call(functools.partial(finish_kernel, first, len(mixed)), out_s...  10 us
    ppermute x14, waiting for transfers between devices, exchange(): arrived.append(lax.ppermute(parts[slot], 'frame', pairs))  7.04 us
    pallas_call x1, Pallas kernels, keys_and_values(): pl.pallas_call(keys_values_kernel, out_shape=(jax.ShapeDtypeStruct((head_...  5.79 us
    ppermute x1, starting transfers between devices, from_behind(): lax.ppermute(value, axis, [(source, source + steps) for source in range(i...  3.36 us
  transfers between devices with their start and end apart: 19, of which 5 were waited for; matrix products, arithmetic and copies ran while one was open for 0% of the time, Pallas kernels for 33%

profile of v1, /device:TPU:0, one launch (start us, length us, event | category | flops | bytes accessed | tf_op | source)
XLA Modules:
  0.0 121.0 jit_solution(8714479177005629412)
XLA Ops:
  1.9 0.7 broadcast_in_dim.39.mod_table
  2.7 0.0 copy-start.5
  2.7 0.6 copy-done.5
  3.3 5.8 %keys_and_values.1 = (bf16[8,768,128]{2,1,0:T(8,128)(2,1)S(1)}, bf16[8,80,768]{2,1,0:T(8,128)(2,1)S(1)}, bf16[768,1152]{1,0:T(8,128)(2,1)S(1)}, f32[1,3456]{1,0:T(1,128)S(1)}, f32[1,1152]{1,0:T(1,128)S(1)}) custom-call(s32[1]{0:T(128)S(6)} %copy.23.level, s32[32]{0:T(128)S(1)} %copy-done.5, s32[1]{0:T(128)S(6)} %copy.24.offset, s32[1]{0:T(128)} %bitcast.frame, ...), custom_call_target="tpu_custom_call" | custom-call | flops 5000000000 | bytes 1048576 | tf_op jit(solution)/shard_map/keys_and_values/pallas_call | solution.py:145
  9.1 0.0 copy-start
  9.1 0.0 copy-start.2
  9.1 0.6 collective-permute-start
  9.7 0.1 collective-permute-start.1
  9.8 2.9 %project_queries.1.queries_in = bf16[8,128,768]{2,1,0:T(8,128)(2,1)S(1)} custom-call(bf16[768,1152]{1,0:T(8,128)(2,1)S(1)} %get-tuple-element.33.normed, bf16[1728,1152]{1,0:T(8,128)(2,1)} %bitcast.42), custom_call_target="tpu_custom_call" | custom-call | flops 3000000000 | bytes 1048576 | tf_op jit(solution)/shard_map/project_queries/pallas_call | solution.py:186
  12.7 0.0 copy-start.9
  12.7 1.4 %collective-permute-done.1.other_values_in = bf16[8,80,768]{2,1,0:T(8,128)(2,1)S(1)} collective-permute-done((bf16[8,80,768]{2,1,0:T(8,128)(2,1)S(1)}, bf16[8,80,768]{2,1,0:T(8,128)(2,1)S(1)}, u32[]{:S(2)}, u32[]{:S(2)}) %collective-permute-start.1) | collective-permute-done | bytes 983072 | tf_op jit(solution)/shard_map/ppermute | solution.py:589
  14.1 0.0 collective-permute-done.other_keys_in
  14.1 0.0 copy-done
  14.2 0.0 copy-done.2
  14.2 8.4 %attend.3 = (f32[256,1152]{1,0:T(8,128)}, bf16[256,1152]{1,0:T(8,128)(2,1)}) custom-call(s32[1]{0:T(128)} %bitcast.frame, bf16[768,1152]{1,0:T(8,128)(2,1)} %bitcast.46, bf16[8,128,768]{2,1,0:T(8,128)(2,1)S(1)} %project_queries.1.queries_in, bf16[8,768,128]{2,1,0:T(8,128)(2,1)S(1)} %get-tuple-element.34.keys_in, ...), custom_call_target="tpu_custom_call" | custom-call | flops 7168000000 | bytes 1048576 | tf_op jit(solution)/shard_map/attend/pallas_call | solution.py:331
  22.6 0.0 copy-done.9
  22.6 0.0 copy-done.3
  22.6 0.0 copy-done.1
  22.6 7.2 %all-to-all-start = ((bf16[8,32,1152]{2,1,0:T(8,128)(2,1)}), bf16[8,32,1152]{2,1,0:T(8,128)(2,1)S(1)}, u32[]{:S(2)}, u32[]{:S(2)}) async-start(bf16[8,32,1152]{2,1,0:T(8,128)(2,1)} %bitcast.40), calls=%async_computation | async-start | bytes 1179648 | tf_op jit(solution)/shard_map/all_to_all | solution.py:552
  29.9 15.3 %attend.2 = (f32[512,1152]{1,0:T(8,128)}, bf16[64,1152]{1,0:T(8,128)(2,1)}, bf16[64,1152]{1,0:T(8,128)(2,1)}, bf16[64,1152]{1,0:T(8,128)(2,1)}, bf16[64,1152]{1,...) custom-call(s32[1]{0:T(128)} %bitcast.frame, ...), custom_call_target="tpu_custom_call" | custom-call | flops 14336000000 | bytes 1048576 | tf_op jit(solution)/shard_map/attend/pallas_call | solution.py:331
  45.2 2.1 %collective-permute-start.2 = (bf16[1,64,1152]{2,1,0:T(8,128)(2,1)}, bf16[1,64,1152]{2,1,0:T(8,128)(2,1)S(1)}, u32[]{:S(2)}, u32[]{:S(2)}) collective-permute-start(bf16[1,64,1152]{2,1,0:T(8,128)(2,1)} %bitcast.54), channel_id=1, source_target_pairs={{0,2},{2,0},{4,6},{6,4},{8,10},{10,8},{12,14},{14,12},{1,3},{3,1},... | collective-permute-start | bytes 442376 | tf_op jit(solution)/shard_map/ppermute | solution.py:556
  47.3 1.5 %collective-permute-start.3 = (bf16[1,64,1152]{2,1,0:T(8,128)(2,1)}, bf16[1,64,1152]{2,1,0:T(8,128)(2,1)S(1)}, u32[]{:S(2)}, u32[]{:S(2)}) collective-permute-start(bf16[1,64,1152]{2,1,0:T(8,128)(2,1)} %bitcast.53), channel_id=1, source_target_pairs={{0,4},{2,6},{4,0},{6,2},{8,12},{10,14},{12,8},{14,10},{1,5},{3,7},... | collective-permute-start | bytes 442376 | tf_op jit(solution)/shard_map/ppermute | solution.py:556
  48.8 0.1 collective-permute-start.4
  48.8 2.9 %collective-permute-start.5 = (bf16[1,64,1152]{2,1,0:T(8,128)(2,1)}, bf16[1,64,1152]{2,1,0:T(8,128)(2,1)S(1)}, u32[]{:S(2)}, u32[]{:S(2)}) collective-permute-start(bf16[1,64,1152]{2,1,0:T(8,128)(2,1)} %bitcast.51), channel_id=1, source_target_pairs={{0,8},{2,10},{4,12},{6,14},{8,0},{10,2},{12,4},{14,6},{1,9},{3,11}... | collective-permute-start | bytes 442376 | tf_op jit(solution)/shard_map/ppermute | solution.py:556
  51.7 1.5 %collective-permute-start.6 = (bf16[1,64,1152]{2,1,0:T(8,128)(2,1)}, bf16[1,64,1152]{2,1,0:T(8,128)(2,1)S(1)}, u32[]{:S(2)}, u32[]{:S(2)}) collective-permute-start(bf16[1,64,1152]{2,1,0:T(8,128)(2,1)} %bitcast.50), channel_id=1, source_target_pairs={{0,10},{2,8},{4,14},{6,12},{8,2},{10,0},{12,6},{14,4},{1,11},{3,9}... | collective-permute-start | bytes 442376 | tf_op jit(solution)/shard_map/ppermute | solution.py:556
  53.1 0.0 collective-permute-done.2.refs_1_
  53.1 3.3 %collective-permute-start.7 = (bf16[1,64,1152]{2,1,0:T(8,128)(2,1)}, bf16[1,64,1152]{2,1,0:T(8,128)(2,1)S(1)}, u32[]{:S(2)}, u32[]{:S(2)}) collective-permute-start(bf16[1,64,1152]{2,1,0:T(8,128)(2,1)} %bitcast.49), channel_id=1, source_target_pairs={{0,12},{2,14},{4,8},{6,10},{8,4},{10,6},{12,0},{14,2},{1,13},{3,15... | collective-permute-start | bytes 442376 | tf_op jit(solution)/shard_map/ppermute | solution.py:556
  56.4 3.0 %collective-permute-done.3.refs_2_ = bf16[1,64,1152]{2,1,0:T(8,128)(2,1)S(1)} collective-permute-done((bf16[1,64,1152]{2,1,0:T(8,128)(2,1)}, bf16[1,64,1152]{2,1,0:T(8,128)(2,1)S(1)}, u32[]{:S(2)}, u32[]{:S(2)}) %collective-permute-start.3) | collective-permute-done | bytes 147488 | tf_op jit(solution)/shard_map/ppermute | solution.py:556
  59.4 0.7 collective-permute-start.8
  60.1 0.0 all-to-all-done.refs_0_
  60.1 6.9 %mix_frames.3 = bf16[8,32,576]{2,1,0:T(8,128)(2,1)} custom-call(bf16[8,32,1152]{2,1,0:T(8,128)(2,1)S(1)} %all-to-all-done.refs_0_, bf16[1728,1152]{1,0:T(8,128)(2,1)} %bitcast.43, f32[512,1152]{1,0:T(8,128)} %get-tuple-element.38.refs_9_.refs_2_.residual_far), custom_call_target="tpu_custom_call" | custom-call | flops 6400000000 | bytes 1048576 | tf_op jit(solution)/shard_map/mix_frames/pallas_call | solution.py:418
  67.0 5.3 %all-to-all-start.1 = ((bf16[8,32,576]{2,1,0:T(8,128)(2,1)}), bf16[8,32,576]{2,1,0:T(8,128)(2,1)S(1)}, u32[]{:S(2)}, u32[]{:S(2)}) async-start(bf16[8,32,576]{2,1,0:T(8,128)(2,1)} %mix_frames.3), calls=%async_computation.1 | async-start | bytes 655360 | tf_op jit(solution)/shard_map/all_to_all | solution.py:552
  72.3 0.0 collective-permute-done.4.refs_3_
  72.3 0.0 collective-permute-done.5.refs_4_
  72.3 3.3 %collective-permute-done.6.refs_5_ = bf16[1,64,1152]{2,1,0:T(8,128)(2,1)S(1)} collective-permute-done((bf16[1,64,1152]{2,1,0:T(8,128)(2,1)}, bf16[1,64,1152]{2,1,0:T(8,128)(2,1)S(1)}, u32[]{:S(2)}, u32[]{:S(2)}) %collective-permute-start.6) | collective-permute-done | bytes 147488 | tf_op jit(solution)/shard_map/ppermute | solution.py:556
  75.6 0.0 collective-permute-done.7.refs_6_
  75.6 0.0 collective-permute-done.8.refs_7_
  75.6 0.0 copy-start.11
  75.6 0.0 copy-start.4
  75.6 0.0 copy-start.6
  75.7 10.4 %mix_frames.2 = (bf16[1,64,576]{2,1,0:T(8,128)(2,1)}, bf16[1,64,576]{2,1,0:T(8,128)(2,1)}, bf16[1,64,576]{2,1,0:T(8,128)(2,1)}, bf16[1,64,576]{2,1,0:T(8,128)(2,...) custom-call(bf16[1,64,1152]{2,1,0:T(8,128)(2,1)S(1)} %bitcast.38, ...), custom_call_target="tpu_custom_call" | custom-call | flops 6400000000 | bytes 1048576 | tf_op jit(solution)/shard_map/mix_frames/pallas_call | solution.py:418
  86.1 0.1 collective-permute-start.9
  86.2 8.7 %collective-permute-start.10 = (bf16[1,64,576]{2,1,0:T(8,128)(2,1)}, bf16[1,64,576]{2,1,0:T(8,128)(2,1)S(1)}, u32[]{:S(2)}, u32[]{:S(2)}) collective-permute-start(bf16[1,64,576]{2,1,0:T(8,128)(2,1)} %get-tuple-element.49), channel_id=1, source_target_pairs={{0,4},{2,6},{4,0},{6,2},{8,12},{10,14},{12,8},{14,10},{1,5},{3,7},... | collective-permute-start | bytes 221192 | tf_op jit(solution)/shard_map/ppermute | solution.py:556
  94.9 1.4 %collective-permute-start.11 = (bf16[1,64,576]{2,1,0:T(8,128)(2,1)}, bf16[1,64,576]{2,1,0:T(8,128)(2,1)S(1)}, u32[]{:S(2)}, u32[]{:S(2)}) collective-permute-start(bf16[1,64,576]{2,1,0:T(8,128)(2,1)} %get-tuple-element.50), channel_id=1, source_target_pairs={{0,6},{2,4},{4,2},{6,0},{8,14},{10,12},{12,10},{14,8},{1,7},{3,5},... | collective-permute-start | bytes 221192 | tf_op jit(solution)/shard_map/ppermute | solution.py:556
  96.3 3.3 %collective-permute-start.12 = (bf16[1,64,576]{2,1,0:T(8,128)(2,1)}, bf16[1,64,576]{2,1,0:T(8,128)(2,1)S(1)}, u32[]{:S(2)}, u32[]{:S(2)}) collective-permute-start(bf16[1,64,576]{2,1,0:T(8,128)(2,1)} %get-tuple-element.51), channel_id=1, source_target_pairs={{0,8},{2,10},{4,12},{6,14},{8,0},{10,2},{12,4},{14,6},{1,9},{3,11}... | collective-permute-start | bytes 221192 | tf_op jit(solution)/shard_map/ppermute | solution.py:556
  99.6 0.0 collective-permute-start.13
  99.6 0.0 collective-permute-done.9
  99.6 2.4 %collective-permute-start.14 = (bf16[1,64,576]{2,1,0:T(8,128)(2,1)}, bf16[1,64,576]{2,1,0:T(8,128)(2,1)S(1)}, u32[]{:S(2)}, u32[]{:S(2)}) collective-permute-start(bf16[1,64,576]{2,1,0:T(8,128)(2,1)} %get-tuple-element.53), channel_id=1, source_target_pairs={{0,12},{2,14},{4,8},{6,10},{8,4},{10,6},{12,0},{14,2},{1,13},{3,15... | collective-permute-start | bytes 221192 | tf_op jit(solution)/shard_map/ppermute | solution.py:556
  102.1 0.0 collective-permute-done.10
  102.1 2.3 %collective-permute-start.15 = (bf16[1,64,576]{2,1,0:T(8,128)(2,1)}, bf16[1,64,576]{2,1,0:T(8,128)(2,1)S(1)}, u32[]{:S(2)}, u32[]{:S(2)}) collective-permute-start(bf16[1,64,576]{2,1,0:T(8,128)(2,1)} %get-tuple-element.54), channel_id=1, source_target_pairs={{0,14},{2,12},{4,10},{6,8},{8,6},{10,4},{12,2},{14,0},{1,15},{3,13... | collective-permute-start | bytes 221192 | tf_op jit(solution)/shard_map/ppermute | solution.py:556
  104.4 0.0 all-to-all-done.1
  104.4 0.0 copy-done.4
  104.4 4.3 %finish.2 = (bf16[768,1152]{1,0:T(8,128)(2,1)}, f32[96,128]{1,0:T(8,128)}, bf16[96,128]{1,0:T(8,128)(2,1)}) custom-call(s32[1]{0:T(128)S(6)} %copy.23.level, s32[32]{0:T(128)S(1)} %copy-done.6, s32[1]{0:T(128)} %bitcast.frame, f32[256,1152]{1,0:T(8,128)} %get-tuple-element.55.residual_far, bf16[576,1152]{1,0:T(8,128)(2,1)} %weight_far.7, ...), custom_call_target="tpu_custom_call" | custom-call | flops 3072000000 | bytes 1048576 | tf_op jit(solution)/shard_map/finish/pallas_call | solution.py:503
  108.7 0.0 collective-permute-done.11
  108.7 0.0 collective-permute-done.12
  108.7 0.0 collective-permute-done.13
  108.7 0.0 collective-permute-done.14
  108.8 0.8 collective-permute-done.15
  109.5 0.0 copy-done.8
  109.5 5.7 %finish.3 = (bf16[768,1152]{1,0:T(8,128)(2,1)}, f32[96,128]{1,0:T(8,128)}, bf16[96,128]{1,0:T(8,128)(2,1)}) custom-call(s32[1]{0:T(128)S(6)} %copy.23.level, s32[32]{0:T(128)S(1)} %copy-done.6, s32[1]{0:T(128)} %bitcast.frame, ...), custom_call_target="tpu_custom_call", output_to_operand_aliasing={{0}: (17, {}), {1}: (18, {}), {2}: (19, {})} | custom-call | flops 6144000000 | bytes 1048576 | tf_op jit(solution)/shard_map/finish/pallas_call | solution.py:503
  115.3 3.4 %collective-permute-start.16 = (bf16[96,128]{1,0:T(8,128)(2,1)}, bf16[96,128]{1,0:T(8,128)(2,1)S(1)}, u32[]{:S(2)}, u32[]{:S(2)}) collective-permute-start(bf16[96,128]{1,0:T(8,128)(2,1)} %get-tuple-element.62), channel_id=1, source_target_pairs={{0,2},{2,4},{4,6},{6,8},{8,10},{10,12},{12,14},{1,3},{3,5},{5,7},{... | collective-permute-start | bytes 73736 | tf_op jit(solution)/shard_map/ppermute | solution.py:36
  118.6 1.7 %collective-permute-done.16 = bf16[96,128]{1,0:T(8,128)(2,1)S(1)} collective-permute-done((bf16[96,128]{1,0:T(8,128)(2,1)}, bf16[96,128]{1,0:T(8,128)(2,1)S(1)}, u32[]{:S(2)}, u32[]{:S(2)}) %collective-permute-start.16) | collective-permute-done | bytes 24608 | tf_op jit(solution)/shard_map/ppermute | solution.py:36
  120.3 0.0 copy-done.10
  120.3 0.6 select_bitcast_fusion
  (9 shorter events, 0.0 us)
Async XLA Ops:
  2.7 0.7 copy-start.5
  9.1 5.0 %copy-start = (bf16[8,768,128]{2,1,0:T(8,128)(2,1)}, bf16[8,768,128]{2,1,0:T(8,128)(2,1)S(1)}, u32[]{:S(2)}) copy-start(bf16[8,768,128]{2,1,0:T(8,128)(2,1)S(1)} %get-tuple-element.34.keys_in) | copy-start | bytes 4718596
  9.1 5.0 %copy-start.2 = (bf16[8,80,768]{2,1,0:T(8,128)(2,1)}, bf16[8,80,768]{2,1,0:T(8,128)(2,1)S(1)}, u32[]{:S(2)}) copy-start(bf16[8,80,768]{2,1,0:T(8,128)(2,1)S(1)} %get-tuple-element.35.values_in) | copy-start | bytes 2949124
  9.1 5.0 %collective-permute-start = (bf16[8,768,128]{2,1,0:T(8,128)(2,1)S(1)}, bf16[8,768,128]{2,1,0:T(8,128)(2,1)S(1)}, u32[]{:S(2)}, u32[]{:S(2)}) collective-permute-start(bf16[8,768,128]{2,1,0:T(8,128)(2,1)S(1)} %get-tuple-element.34.keys_in), channel_id=1, source_target_pairs={{0,1},{1,0},{2,3},{3,2},{4,5},{5,4},{6,7},{7,6},{8,9},{9,8},{10,11... | collective-permute-start | bytes 4718600 | tf_op jit(solution)/shard_map/ppermute | solution.py:589
  9.7 4.4 %collective-permute-start.1 = (bf16[8,80,768]{2,1,0:T(8,128)(2,1)S(1)}, bf16[8,80,768]{2,1,0:T(8,128)(2,1)S(1)}, u32[]{:S(2)}, u32[]{:S(2)}) collective-permute-start(bf16[8,80,768]{2,1,0:T(8,128)(2,1)S(1)} %get-tuple-element.35.values_in), channel_id=1, source_target_pairs={{0,1},{1,0},{2,3},{3,2},{4,5},{5,4},{6,7},{7,6},{8,9},{9,8},{10,11... | collective-permute-start | bytes 2949128 | tf_op jit(solution)/shard_map/ppermute | solution.py:589
  12.7 9.9 %copy-start.9 = (bf16[8,128,768]{2,1,0:T(8,128)(2,1)}, bf16[8,128,768]{2,1,0:T(8,128)(2,1)S(1)}, u32[]{:S(2)}) copy-start(bf16[8,128,768]{2,1,0:T(8,128)(2,1)S(1)} %project_queries.1.queries_in) | copy-start | bytes 4718596
  14.1 8.5 %copy-start.3 = (bf16[8,80,768]{2,1,0:T(8,128)(2,1)}, bf16[8,80,768]{2,1,0:T(8,128)(2,1)S(1)}, u32[]{:S(2)}) copy-start(bf16[8,80,768]{2,1,0:T(8,128)(2,1)S(1)} %collective-permute-done.1.other_values_in) | copy-start | bytes 2949124
  14.1 8.5 %copy-start.1 = (bf16[8,768,128]{2,1,0:T(8,128)(2,1)}, bf16[8,768,128]{2,1,0:T(8,128)(2,1)S(1)}, u32[]{:S(2)}) copy-start(bf16[8,768,128]{2,1,0:T(8,128)(2,1)S(1)} %collective-permute-done.other_keys_in) | copy-start | bytes 4718596
  22.6 37.5 %all-to-all-start = ((bf16[8,32,1152]{2,1,0:T(8,128)(2,1)}), bf16[8,32,1152]{2,1,0:T(8,128)(2,1)S(1)}, u32[]{:S(2)}, u32[]{:S(2)}) async-start(bf16[8,32,1152]{2,1,0:T(8,128)(2,1)} %bitcast.40), calls=%async_computation | async-start | bytes 1179648 | tf_op jit(solution)/shard_map/all_to_all | solution.py:552
  45.2 7.9 %collective-permute-start.2 = (bf16[1,64,1152]{2,1,0:T(8,128)(2,1)}, bf16[1,64,1152]{2,1,0:T(8,128)(2,1)S(1)}, u32[]{:S(2)}, u32[]{:S(2)}) collective-permute-start(bf16[1,64,1152]{2,1,0:T(8,128)(2,1)} %bitcast.54), channel_id=1, source_target_pairs={{0,2},{2,0},{4,6},{6,4},{8,10},{10,8},{12,14},{14,12},{1,3},{3,1},... | collective-permute-start | bytes 442376 | tf_op jit(solution)/shard_map/ppermute | solution.py:556
  47.3 12.1 %collective-permute-start.3 = (bf16[1,64,1152]{2,1,0:T(8,128)(2,1)}, bf16[1,64,1152]{2,1,0:T(8,128)(2,1)S(1)}, u32[]{:S(2)}, u32[]{:S(2)}) collective-permute-start(bf16[1,64,1152]{2,1,0:T(8,128)(2,1)} %bitcast.53), channel_id=1, source_target_pairs={{0,4},{2,6},{4,0},{6,2},{8,12},{10,14},{12,8},{14,10},{1,5},{3,7},... | collective-permute-start | bytes 442376 | tf_op jit(solution)/shard_map/ppermute | solution.py:556
  48.8 23.5 %collective-permute-start.4 = (bf16[1,64,1152]{2,1,0:T(8,128)(2,1)}, bf16[1,64,1152]{2,1,0:T(8,128)(2,1)S(1)}, u32[]{:S(2)}, u32[]{:S(2)}) collective-permute-start(bf16[1,64,1152]{2,1,0:T(8,128)(2,1)} %bitcast.52), channel_id=1, source_target_pairs={{0,6},{2,4},{4,2},{6,0},{8,14},{10,12},{12,10},{14,8},{1,7},{3,5},... | collective-permute-start | bytes 442376 | tf_op jit(solution)/shard_map/ppermute | solution.py:556
  48.8 23.5 %collective-permute-start.5 = (bf16[1,64,1152]{2,1,0:T(8,128)(2,1)}, bf16[1,64,1152]{2,1,0:T(8,128)(2,1)S(1)}, u32[]{:S(2)}, u32[]{:S(2)}) collective-permute-start(bf16[1,64,1152]{2,1,0:T(8,128)(2,1)} %bitcast.51), channel_id=1, source_target_pairs={{0,8},{2,10},{4,12},{6,14},{8,0},{10,2},{12,4},{14,6},{1,9},{3,11}... | collective-permute-start | bytes 442376 | tf_op jit(solution)/shard_map/ppermute | solution.py:556
  51.7 23.9 %collective-permute-start.6 = (bf16[1,64,1152]{2,1,0:T(8,128)(2,1)}, bf16[1,64,1152]{2,1,0:T(8,128)(2,1)S(1)}, u32[]{:S(2)}, u32[]{:S(2)}) collective-permute-start(bf16[1,64,1152]{2,1,0:T(8,128)(2,1)} %bitcast.50), channel_id=1, source_target_pairs={{0,10},{2,8},{4,14},{6,12},{8,2},{10,0},{12,6},{14,4},{1,11},{3,9}... | collective-permute-start | bytes 442376 | tf_op jit(solution)/shard_map/ppermute | solution.py:556
  53.1 22.5 %collective-permute-start.7 = (bf16[1,64,1152]{2,1,0:T(8,128)(2,1)}, bf16[1,64,1152]{2,1,0:T(8,128)(2,1)S(1)}, u32[]{:S(2)}, u32[]{:S(2)}) collective-permute-start(bf16[1,64,1152]{2,1,0:T(8,128)(2,1)} %bitcast.49), channel_id=1, source_target_pairs={{0,12},{2,14},{4,8},{6,10},{8,4},{10,6},{12,0},{14,2},{1,13},{3,15... | collective-permute-start | bytes 442376 | tf_op jit(solution)/shard_map/ppermute | solution.py:556
  59.4 16.2 %collective-permute-start.8 = (bf16[1,64,1152]{2,1,0:T(8,128)(2,1)}, bf16[1,64,1152]{2,1,0:T(8,128)(2,1)S(1)}, u32[]{:S(2)}, u32[]{:S(2)}) collective-permute-start(bf16[1,64,1152]{2,1,0:T(8,128)(2,1)} %bitcast.48), channel_id=1, source_target_pairs={{0,14},{2,12},{4,10},{6,8},{8,6},{10,4},{12,2},{14,0},{1,15},{3,13... | collective-permute-start | bytes 442376 | tf_op jit(solution)/shard_map/ppermute | solution.py:556
  60.1 15.5 %copy-start.7 = (bf16[64,1152]{1,0:T(8,128)(2,1)S(1)}, bf16[64,1152]{1,0:T(8,128)(2,1)}, u32[]{:S(2)}) copy-start(bf16[64,1152]{1,0:T(8,128)(2,1)} %get-tuple-element.39) | copy-start | bytes 442372
  67.0 37.3 %all-to-all-start.1 = ((bf16[8,32,576]{2,1,0:T(8,128)(2,1)}), bf16[8,32,576]{2,1,0:T(8,128)(2,1)S(1)}, u32[]{:S(2)}, u32[]{:S(2)}) async-start(bf16[8,32,576]{2,1,0:T(8,128)(2,1)} %mix_frames.3), calls=%async_computation.1 | async-start | bytes 655360 | tf_op jit(solution)/shard_map/all_to_all | solution.py:552
  75.6 19.3 %copy-start.11 = (f32[1152]{0:T(1024)S(1)}, f32[1152]{0:T(1024)}, u32[]{:S(2)}) copy-start(f32[1152]{0:T(1024)} %param.26) | copy-start | bytes 13828
  75.6 28.7 %copy-start.4 = (bf16[1152,16]{0,1:T(8,128)(2,1)S(1)}, bf16[1152,16]{0,1:T(8,128)(2,1)}, u32[]{:S(2)}) copy-start(bf16[1152,16]{0,1:T(8,128)(2,1)} %param.27) | copy-start | bytes 110596
  75.6 28.7 %copy-start.6 = (s32[32]{0:T(128)S(1)}, s32[32]{0:T(128)}, u32[]{:S(2)}) copy-start(s32[32]{0:T(128)} %table.5) | copy-start | bytes 388
  86.1 13.5 %collective-permute-start.9 = (bf16[1,64,576]{2,1,0:T(8,128)(2,1)}, bf16[1,64,576]{2,1,0:T(8,128)(2,1)S(1)}, u32[]{:S(2)}, u32[]{:S(2)}) collective-permute-start(bf16[1,64,576]{2,1,0:T(8,128)(2,1)} %get-tuple-element.48), channel_id=1, source_target_pairs={{0,2},{2,0},{4,6},{6,4},{8,10},{10,8},{12,14},{14,12},{1,3},{3,1},... | collective-permute-start | bytes 221192 | tf_op jit(solution)/shard_map/ppermute | solution.py:556
  86.2 15.9 %collective-permute-start.10 = (bf16[1,64,576]{2,1,0:T(8,128)(2,1)}, bf16[1,64,576]{2,1,0:T(8,128)(2,1)S(1)}, u32[]{:S(2)}, u32[]{:S(2)}) collective-permute-start(bf16[1,64,576]{2,1,0:T(8,128)(2,1)} %get-tuple-element.49), channel_id=1, source_target_pairs={{0,4},{2,6},{4,0},{6,2},{8,12},{10,14},{12,8},{14,10},{1,5},{3,7},... | collective-permute-start | bytes 221192 | tf_op jit(solution)/shard_map/ppermute | solution.py:556
  94.9 13.8 %collective-permute-start.11 = (bf16[1,64,576]{2,1,0:T(8,128)(2,1)}, bf16[1,64,576]{2,1,0:T(8,128)(2,1)S(1)}, u32[]{:S(2)}, u32[]{:S(2)}) collective-permute-start(bf16[1,64,576]{2,1,0:T(8,128)(2,1)} %get-tuple-element.50), channel_id=1, source_target_pairs={{0,6},{2,4},{4,2},{6,0},{8,14},{10,12},{12,10},{14,8},{1,7},{3,5},... | collective-permute-start | bytes 221192 | tf_op jit(solution)/shard_map/ppermute | solution.py:556
  96.3 12.4 %collective-permute-start.12 = (bf16[1,64,576]{2,1,0:T(8,128)(2,1)}, bf16[1,64,576]{2,1,0:T(8,128)(2,1)S(1)}, u32[]{:S(2)}, u32[]{:S(2)}) collective-permute-start(bf16[1,64,576]{2,1,0:T(8,128)(2,1)} %get-tuple-element.51), channel_id=1, source_target_pairs={{0,8},{2,10},{4,12},{6,14},{8,0},{10,2},{12,4},{14,6},{1,9},{3,11}... | collective-permute-start | bytes 221192 | tf_op jit(solution)/shard_map/ppermute | solution.py:556
  99.6 9.1 %collective-permute-start.13 = (bf16[1,64,576]{2,1,0:T(8,128)(2,1)}, bf16[1,64,576]{2,1,0:T(8,128)(2,1)S(1)}, u32[]{:S(2)}, u32[]{:S(2)}) collective-permute-start(bf16[1,64,576]{2,1,0:T(8,128)(2,1)} %get-tuple-element.52), channel_id=1, source_target_pairs={{0,10},{2,8},{4,14},{6,12},{8,2},{10,0},{12,6},{14,4},{1,11},{3,9}... | collective-permute-start | bytes 221192 | tf_op jit(solution)/shard_map/ppermute | solution.py:556
  99.6 9.1 %collective-permute-start.14 = (bf16[1,64,576]{2,1,0:T(8,128)(2,1)}, bf16[1,64,576]{2,1,0:T(8,128)(2,1)S(1)}, u32[]{:S(2)}, u32[]{:S(2)}) collective-permute-start(bf16[1,64,576]{2,1,0:T(8,128)(2,1)} %get-tuple-element.53), channel_id=1, source_target_pairs={{0,12},{2,14},{4,8},{6,10},{8,4},{10,6},{12,0},{14,2},{1,13},{3,15... | collective-permute-start | bytes 221192 | tf_op jit(solution)/shard_map/ppermute | solution.py:556
  102.1 7.5 %collective-permute-start.15 = (bf16[1,64,576]{2,1,0:T(8,128)(2,1)}, bf16[1,64,576]{2,1,0:T(8,128)(2,1)S(1)}, u32[]{:S(2)}, u32[]{:S(2)}) collective-permute-start(bf16[1,64,576]{2,1,0:T(8,128)(2,1)} %get-tuple-element.54), channel_id=1, source_target_pairs={{0,14},{2,12},{4,10},{6,8},{8,6},{10,4},{12,2},{14,0},{1,15},{3,13... | collective-permute-start | bytes 221192 | tf_op jit(solution)/shard_map/ppermute | solution.py:556
  104.4 5.2 %copy-start.8 = (bf16[1,64,576]{2,1,0:T(8,128)(2,1)S(1)}, bf16[1,64,576]{2,1,0:T(8,128)(2,1)}, u32[]{:S(2)}) copy-start(bf16[1,64,576]{2,1,0:T(8,128)(2,1)} %get-tuple-element.47) | copy-start | bytes 221188
  109.5 10.8 %copy-start.10 = (f32[96,128]{1,0:T(8,128)S(1)}, f32[96,128]{1,0:T(8,128)}, u32[]{:S(2)}) copy-start(f32[96,128]{1,0:T(8,128)} %param.16) | copy-start | bytes 147460
  115.3 5.1 %collective-permute-start.16 = (bf16[96,128]{1,0:T(8,128)(2,1)}, bf16[96,128]{1,0:T(8,128)(2,1)S(1)}, u32[]{:S(2)}, u32[]{:S(2)}) collective-permute-start(bf16[96,128]{1,0:T(8,128)(2,1)} %get-tuple-element.62), channel_id=1, source_target_pairs={{0,2},{2,4},{4,6},{6,8},{8,10},{10,12},{12,14},{1,3},{3,5},{5,7},{... | collective-permute-start | bytes 73736 | tf_op jit(solution)/shard_map/ppermute | solution.py:36

commit v2 on v1

--- a/solution.py
+++ b/solution.py
@@ -15,9 +15,10 @@
 PADDED = 128
 LANES = 128
 QUERY_BLOCK = 256
+KEY_BLOCK = 256
 
 epsilon = 1e-06
-scale_of_scores = 1.0 / math.sqrt(HEAD_SIZE)
+scale_of_scores = math.log2(math.e) / math.sqrt(HEAD_SIZE)
 
 WHOLE = pl.BlockSpec(memory_space=pltpu.VMEM)
 SCALARS = pl.BlockSpec(memory_space=pltpu.SMEM)
@@ -90,13 +91,16 @@
 
 
 def keys_values_kernel(
-    level, table, offset, frame, hidden_far, mod_table, time_far, weight_far,
-    keys, values, normed, modulation, placed,
-    hidden, time_weight, weight, sems,
+    level, offset, frame, table_far, hidden_far, mod_far, time_far, weight_far,
+    keys, values, normed, modulation, placed, delta,
+    hidden, time_weight, weight, mod_table, table, sems,
 ):
     rows_total, width = hidden.shape
     head_count = keys.shape[0]
     attended = head_count * HEAD_SIZE
+    table_copy = pltpu.make_async_copy(table_far, table, sems.at[4])
+    mod_copy = pltpu.make_async_copy(mod_far, mod_table, sems.at[5])
+    start_all([table_copy, mod_copy])
     time_copy = pltpu.make_async_copy(time_far, time_weight, sems.at[0])
     hidden_copy = pltpu.make_async_copy(hidden_far, hidden, sems.at[1])
     weight_copies = [
@@ -108,17 +112,22 @@
         for part in range(2)
     ]
     start_all([time_copy, hidden_copy] + weight_copies)
+    placed[...] = sinusoid_row(
+        (frame[0] + offset[0]).astype(jnp.float32), width, width // 2, True
+    )
+    table_copy.wait()
     now = table[level[0]].astype(jnp.float32)
+    following = table[level[0] - 1].astype(jnp.float32)
+    delta[...] = jnp.full(delta.shape, (following - now) / 1000.0, jnp.float32)
     frequencies = time_weight.shape[0]
     embedded = sinusoid_row(now, frequencies, frequencies // 2, False)
     activated = (embedded * (1.0 / (1.0 + jnp.exp(-embedded)))).astype(jnp.bfloat16)
     spread = jnp.broadcast_to(activated.astype(jnp.float32), (16, frequencies)).astype(jnp.bfloat16)
-    placed[...] = sinusoid_row(
-        (frame[0] + offset[0]).astype(jnp.float32), width, width // 2, True
-    )
+    mod_copy.wait()
     time_copy.wait()
     projected = jnp.dot(spread, time_weight[...], preferred_element_type=jnp.float32)
-    modulation[...] = mod_table[...] + projected[:1, :]
+    lined = jnp.concatenate([mod_table[row : row + 1, :] for row in range(mod_table.shape[0])], axis=1)
+    modulation[...] = lined + projected[:1, :]
     shift = modulation[:, :width]
     scale = 1.0 + modulation[:, width : 2 * width]
     hidden_copy.wait()
@@ -141,28 +150,31 @@
 
 def keys_and_values(level, table, offset, frame, hidden, mod_table, time_weight, weight, head_count):
     rows, width = hidden.shape
-    hidden, time_weight, weight = in_hbm(hidden, time_weight, weight)
+    far = in_hbm(table, hidden, mod_table, time_weight, weight)
     return pl.pallas_call(
         keys_values_kernel,
         out_shape=(
             jax.ShapeDtypeStruct((head_count, rows, PADDED), jnp.bfloat16),
             jax.ShapeDtypeStruct((head_count, VALUE_ROWS, rows), jnp.bfloat16),
             jax.ShapeDtypeStruct((rows, width), jnp.bfloat16),
-            jax.ShapeDtypeStruct(mod_table.shape, jnp.float32),
+            jax.ShapeDtypeStruct((1, mod_table.size), jnp.float32),
             jax.ShapeDtypeStruct((1, width), jnp.float32),
+            jax.ShapeDtypeStruct((1, LANES), jnp.float32),
         ),
-        in_specs=[SCALARS] * 4 + [REMAIN, WHOLE, REMAIN, REMAIN],
-        out_specs=(WHOLE,) * 5,
+        in_specs=[SCALARS] * 3 + [REMAIN] * 5,
+        out_specs=(WHOLE,) * 6,
         scratch_shapes=[
             pltpu.VMEM(hidden.shape, jnp.bfloat16),
             pltpu.VMEM(time_weight.shape, jnp.bfloat16),
             pltpu.VMEM((2 * head_count * HEAD_SIZE, width), jnp.bfloat16),
-            pltpu.SemaphoreType.DMA((4,)),
+            pltpu.VMEM(mod_table.shape, jnp.float32),
+            pltpu.SMEM(table.shape, jnp.int32),
+            pltpu.SemaphoreType.DMA((6,)),
         ],
         compiler_params=PARAMS,
         cost_estimate=cost(5),
         name="keys_and_values",
-    )(level, table, offset, frame, hidden, mod_table, time_weight, weight)
+    )(level, offset, frame, *far)
 
 
 def queries_kernel(normed, weight_far, queries, weight, sems):
@@ -245,42 +257,67 @@
     queries, keys, values, other_keys, other_values = near
     stored = 2 + len(loaded) * head_count
     begin = first if resident else 0
-    turned[attended:, :] = jnp.zeros((turned.shape[0] - attended, QUERY_BLOCK), jnp.float32)
+    block = scores_a.shape[1]
+    turned[attended:, :] = jnp.zeros((turned.shape[0] - attended, block), jnp.float32)
     stores = []
-    for start in range(0, count, QUERY_BLOCK):
-        span = slice(begin + start, begin + start + QUERY_BLOCK)
-
-        def one(head, scores):
-            query = queries[head, :, span]
-            own = jnp.dot(keys[head], query, preferred_element_type=jnp.float32)
-            scores[:half, :] = own
-            top = jnp.max(own, axis=0, keepdims=True)
-            other = jnp.dot(other_keys[head], query, preferred_element_type=jnp.float32)
-            scores[half:, :] = other
-            top = jnp.maximum(top, jnp.max(other, axis=0, keepdims=True))
-            weights = jnp.exp(scores[:half, :] - top).astype(jnp.bfloat16)
-            total = jnp.dot(values[head], weights, preferred_element_type=jnp.float32)
-            weights = jnp.exp(scores[half:, :] - top).astype(jnp.bfloat16)
-            total += jnp.dot(other_values[head], weights, preferred_element_type=jnp.float32)
-            turned[pl.ds(pl.multiple_of(head * HEAD_SIZE, 8), HEAD_SIZE), :] = share_out(total)
-
-        def pair(index, carry):
+    for start in range(0, count, block):
+        span = slice(begin + start, begin + start + block)
+        spots = [
+            (side, key, slice(key, key + KEY_BLOCK), slice(side * half + key, side * half + key + KEY_BLOCK))
+            for side in range(2)
+            for key in range(0, half, KEY_BLOCK)
+        ]
+
+        def arrive(head):
             if start == 0 and not resident:
-                for head in (2 * index, 2 * index + 1):
-                    for copy in head_copies(head):
-                        copy.wait()
-            one(2 * index, scores_a)
-            one(2 * index + 1, scores_b)
-            return carry
-
-        lax.fori_loop(0, head_count // 2, pair, 0)
+                for copy in head_copies(head):
+                    copy.wait()
+
+        def advance(scored, scores, mixed, known, top):
+            highest, total = (None, None)
+            for side, _, local, place in spots:
+                if scored is not None:
+                    part = jnp.dot(
+                        (keys, other_keys)[side][scored, local, :], queries[scored, :, span],
+                        preferred_element_type=jnp.float32,
+                    )
+                    scores[place, :] = part
+                    peak = jnp.max(part, axis=0, keepdims=True)
+                    highest = peak if highest is None else jnp.maximum(highest, peak)
+                if mixed is not None:
+                    weights = jnp.exp2(known[place, :] - top).astype(jnp.bfloat16)
+                    part = jnp.dot(
+                        (values, other_values)[side][mixed, :, local], weights,
+                        preferred_element_type=jnp.float32,
+                    )
+                    total = part if total is None else total + part
+            if mixed is not None:
+                begin_row = mixed * HEAD_SIZE
+                if not isinstance(mixed, int):
+                    begin_row = pl.multiple_of(begin_row, 8)
+                turned[pl.ds(begin_row, HEAD_SIZE), :] = share_out(total)
+            return highest
+
+        def pair(index, top):
+            arrive(2 * index + 1)
+            middle = advance(2 * index + 1, scores_b, 2 * index, scores_a, top)
+            arrive(2 * index + 2)
+            return advance(2 * index + 2, scores_a, 2 * index + 1, scores_b, middle)
+
+        arrive(0)
+        top = lax.fori_loop(
+            0, head_count // 2 - 1, pair, advance(0, scores_a, None, None, None)
+        )
+        arrive(head_count - 1)
+        top = advance(head_count - 1, scores_b, head_count - 2, scores_a, top)
+        advance(None, None, head_count - 1, scores_b, top)
         turn_back(turned, rows, attended)
         if start == 0:
             hidden_copy.wait()
             weight_copy.wait()
         gate = modulation[:, 2 * width :]
         step = QUERY_BLOCK // 2
-        for part in range(0, QUERY_BLOCK, step):
+        for part in range(0, block, step):
             span = slice(start + part, start + part + step)
             term = jnp.dot(
                 rows[part : part + step, :attended], weight[...],
@@ -328,6 +365,7 @@
         )
     sem_count = 2 + len(loaded) * head_count + 4 * (count // QUERY_BLOCK) + slots
     outs = max(slots, 1)
+    block = 2 * QUERY_BLOCK if count % (2 * QUERY_BLOCK) == 0 else QUERY_BLOCK
     return pl.pallas_call(
         functools.partial(attend_kernel, first, resident, slots),
         out_shape=(
@@ -337,10 +375,10 @@
         in_specs=[SCALARS, REMAIN] + [near] * 5 + [REMAIN] + [WHOLE] * 2,
         out_specs=(REMAIN,) * (1 + outs),
         scratch_shapes=[
-            pltpu.VMEM((2 * keys.shape[1], QUERY_BLOCK), jnp.float32),
-            pltpu.VMEM((2 * keys.shape[1], QUERY_BLOCK), jnp.float32),
-            pltpu.VMEM((deep, QUERY_BLOCK), jnp.float32),
-            pltpu.VMEM((QUERY_BLOCK, deep), jnp.bfloat16),
+            pltpu.VMEM((2 * keys.shape[1], block), jnp.float32),
+            pltpu.VMEM((2 * keys.shape[1], block), jnp.float32),
+            pltpu.VMEM((deep, block), jnp.float32),
+            pltpu.VMEM((block, deep), jnp.bfloat16),
             pltpu.VMEM((count, width), jnp.bfloat16),
             pltpu.VMEM(out_weight.shape, jnp.bfloat16),
             pltpu.VMEM((count, width), jnp.float32),
@@ -354,21 +392,23 @@
     )(frame, hidden, queries, keys, values, *other, out_weight, modulation, placed)
 
 
-def temporal_kernel(group, tokens, parts, *refs):
-    gathered, weight_far, mixed = (refs[:parts], refs[parts], refs[-6 - parts : -6])
-    weight, turned, bias, turned_out, rows, sems = refs[-6:]
+def temporal_kernel(group, tokens, parts, frame, *refs):
+    gathered, weight_far, mixed = (refs[:parts], refs[parts], refs[-8])
+    weight, turned, bias, scores, turned_out, rows, sems = refs[-7:]
     frames, share, width = gathered[0].shape
-    attended = mixed[0].shape[2]
+    attended = mixed.shape[2]
     head_count = attended // HEAD_SIZE
     count = bias.shape[0]
+    pieces = sems.shape[0]
+    height = weight.shape[0] // pieces
     weight_copies = start_all(
         [
             pltpu.make_async_copy(
-                weight_far.at[pl.ds(part * attended, attended), :],
-                weight.at[pl.ds(part * attended, attended), :],
-                sems.at[part],
+                weight_far.at[pl.ds(piece * height, height), :],
+                weight.at[pl.ds(piece * height, height), :],
+                sems.at[piece],
             )
-            for part in range(3)
+            for piece in range(pieces)
         ]
     )
     own = lax.rem(lax.broadcasted_iota(jnp.int32, (count, count), 0), tokens)
@@ -380,31 +420,40 @@
             [part[:, start : start + group, :].reshape(frames * group, width) for part in gathered],
             axis=0,
         )
-        for part in range(3):
+        for piece in range(pieces):
             if start == 0:
-                weight_copies[part].wait()
-            span = slice(part * attended, (part + 1) * attended)
+                weight_copies[piece].wait()
+            span = slice(piece * height, (piece + 1) * height)
             turned[span, :] = lax.dot_general(
                 weight[span, :], block, ACROSS, preferred_element_type=jnp.float32
             )
-        for head in range(head_count):
-            query, key, value = (
-                turned[part * attended + head * HEAD_SIZE : part * attended + (head + 1) * HEAD_SIZE, :]
-                for part in range(3)
+        together = scores.shape[0]
+        for begin in range(0, head_count, together):
+            tops = []
+            for place in range(together):
+                first = (begin + place) * HEAD_SIZE
+                query = turned[first : first + HEAD_SIZE, :]
+                key = turned[attended + first : attended + first + HEAD_SIZE, :]
+                found = jnp.dot(as_key(key), as_query(query), preferred_element_type=jnp.float32)
+                found = found + bias[...]
+                scores[place, :, :] = found
+                tops.append(jnp.max(found, axis=0, keepdims=True))
+            for place in range(together):
+                first = (begin + place) * HEAD_SIZE
+                value = turned[2 * attended + first : 2 * attended + first + HEAD_SIZE, :]
+                weights = jnp.exp2(scores[place, :, :] - tops[place]).astype(jnp.bfloat16)
+                total = jnp.dot(as_value(value), weights, preferred_element_type=jnp.float32)
+                turned_out[first : first + HEAD_SIZE, :] = share_out(total)
+        turn_back(turned_out, rows, attended)
+        for slot in range(parts):
+            span = slice(slot * frames * group, (slot + 1) * frames * group)
+            owner = lax.bitwise_xor(frame[0], slot) if parts > 1 else 0
+            mixed[pl.ds(owner, frames), start : start + group, :] = rows[span, :attended].reshape(
+                frames, group, attended
             )
-            scores = jnp.dot(as_key(key), as_query(query), preferred_element_type=jnp.float32)
-            scores = scores + bias[...]
-            top = jnp.max(scores, axis=0, keepdims=True)
-            weights = jnp.exp(scores - top).astype(jnp.bfloat16)
-            total = jnp.dot(as_value(value), weights, preferred_element_type=jnp.float32)
-            turned_out[head * HEAD_SIZE : (head + 1) * HEAD_SIZE, :] = share_out(total)
-        turn_back(turned_out, rows, attended)
-        for place, part in enumerate(mixed):
-            span = slice(place * frames * group, (place + 1) * frames * group)
-            part[:, start : start + group, :] = rows[span, :attended].reshape(frames, group, attended)
-
-
-def mix_frames(gathered, weight, attended, after):
+
+
+def mix_frames(frame, gathered, weight, attended, after):
     parts = len(gathered)
     given = gathered[0].shape
     frames, share, width = given
@@ -414,63 +463,65 @@
     if group == 0 or group % 16 or share % group:
         shape, group, tokens = ((1, frames * share, width), frames * share, share)
     count = parts * shape[0] * group
+    together = attended // HEAD_SIZE if count <= QUERY_BLOCK else 1
     deep = round_up(attended, LANES)
     mixed = pl.pallas_call(
         functools.partial(temporal_kernel, group, tokens, parts),
-        out_shape=(pltpu.HBM(shape[:2] + (attended,), jnp.bfloat16),) * parts,
-        in_specs=[WHOLE] * parts + [REMAIN] * (1 + len(after)),
-        out_specs=(WHOLE,) * parts,
+        out_shape=jax.ShapeDtypeStruct((parts * shape[0], shape[1], attended), jnp.bfloat16),
+        in_specs=[SCALARS] + [WHOLE] * parts + [REMAIN] * (1 + len(after)),
+        out_specs=WHOLE,
         scratch_shapes=[
             pltpu.VMEM(weight.shape, jnp.bfloat16),
             pltpu.VMEM((weight.shape[0], count), jnp.float32),
             pltpu.VMEM((count, count), jnp.float32),
+            pltpu.VMEM((together, count, count), jnp.float32),
             pltpu.VMEM((deep, count), jnp.float32),
             pltpu.VMEM((count, deep), jnp.bfloat16),
-            pltpu.SemaphoreType.DMA((3,)),
+            pltpu.SemaphoreType.DMA((9,)),
         ],
         compiler_params=PARAMS,
         cost_estimate=cost(0.025 * count),
         name="mix_frames",
-    )(*[part.reshape(shape) for part in gathered], *in_hbm(weight, *after))
-    return [part.reshape(given[:2] + (attended,)) for part in mixed]
+    )(frame, *[part.reshape(shape) for part in gathered], *in_hbm(weight, *after))
+    return mixed.reshape(whole, share, attended)
 
 
 def finish_kernel(
-    first, parts, level, table, frame, residual_far, weight_far, modulation, gain, out_weight,
-    latents_far, *refs,
+    first, delta, residual_far, mixed, weight, modulation, gain, out_weight, latents, *refs,
 ):
-    returned = refs[:parts]
-    hidden_far, velocity_far, update_far, residual, weight, latents, hidden, velocity, update, mixed, sems = refs[-11:]
+    hidden_far, velocity_far, update_far, residual, hidden, velocity, update, sems = refs[-8:]
+    blocks = residual.shape[0] // QUERY_BLOCK
+    loads = start_all(
+        [
+            pltpu.make_async_copy(
+                residual_far.at[pl.ds(block * QUERY_BLOCK, QUERY_BLOCK), :],
+                residual.at[pl.ds(block * QUERY_BLOCK, QUERY_BLOCK), :],
+                sems.at[2 + blocks + block],
+            )
+            for block in range(blocks)
+        ]
+    )
     count, width = residual.shape
     channels = out_weight.shape[0]
     fold = LANES // channels
     lines = pl.ds(first // fold, count // fold)
-    weight_copy = pltpu.make_async_copy(weight_far, weight, sems.at[0])
-    residual_copy = pltpu.make_async_copy(residual_far, residual, sems.at[1])
-    latents_copy = pltpu.make_async_copy(latents_far.at[lines, :], latents, sems.at[2])
-    start_all([weight_copy, residual_copy, latents_copy])
     spread = lax.rem(lax.broadcasted_iota(jnp.int32, (LANES, channels), 0), channels)
     spread = jnp.where(
         spread == lax.broadcasted_iota(jnp.int32, (LANES, channels), 1), 1.0, 0.0
     ).astype(jnp.bfloat16)
     repeated = jnp.dot(spread, out_weight[...], preferred_element_type=jnp.float32)
     repeated = repeated.astype(jnp.bfloat16)
-    for slot, part in enumerate(returned):
-        share = part.shape[0]
-        where = lax.bitwise_xor(frame[0], slot) * share if parts > 1 else 0
-        mixed[pl.ds(pl.multiple_of(where, 16), share), :] = part[...]
-    weight_copy.wait()
-    residual_copy.wait()
     stores = []
     for start in range(0, count, QUERY_BLOCK):
         span = slice(start, start + QUERY_BLOCK)
         term = jnp.dot(mixed[span, :], weight[...], preferred_element_type=jnp.float32)
+        loads[start // QUERY_BLOCK].wait()
         block = residual[span, :] + modulation[:, 2 * width :] * term
         hidden[span, :] = block.astype(jnp.bfloat16)
         copy = pltpu.make_async_copy(
             hidden.at[pl.ds(start, QUERY_BLOCK), :],
             hidden_far.at[pl.ds(first + start, QUERY_BLOCK), :],
-            sems.at[5 + len(stores)],
+            sems.at[2 + len(stores)],
         )
         copy.start()
         stores.append(copy)
@@ -480,55 +531,44 @@
         lane = lax.broadcasted_iota(jnp.int32, (QUERY_BLOCK, LANES), 1) // channels
         picked = jnp.where(row == lane, wide, 0.0).reshape(QUERY_BLOCK // fold, fold, LANES)
         velocity[start // fold : (start + QUERY_BLOCK) // fold, :] = jnp.sum(picked, axis=1)
-    now = table[level[0]]
-    following = table[level[0] - 1]
-    delta = (following - now).astype(jnp.float32) / 1000.0
-    latents_copy.wait()
-    update[...] = (latents[...] + delta * velocity[...]).astype(jnp.bfloat16)
+    known = latents[first // fold : (first + count) // fold, :]
+    update[...] = (known + delta[...] * velocity[...]).astype(jnp.bfloat16)
     stores += start_all(
         [
-            pltpu.make_async_copy(velocity, velocity_far.at[lines, :], sems.at[3]),
-            pltpu.make_async_copy(update, update_far.at[lines, :], sems.at[4]),
+            pltpu.make_async_copy(velocity, velocity_far.at[lines, :], sems.at[0]),
+            pltpu.make_async_copy(update, update_far.at[lines, :], sems.at[1]),
         ]
     )
     for copy in stores:
         copy.wait()
 
 
-def finish(first, so_far, level, table, frame, residual, mixed, weight, modulation, gain, out_weight, latents, tokens):
+def finish(first, so_far, delta, residual, mixed, weight, modulation, gain, out_weight, latents, tokens):
     count, width = residual.shape
     lines = count * out_weight.shape[0] // LANES
-    known = 9 + len(mixed)
-    residual, weight, latents = in_hbm(residual, weight, latents)
+    known = 8
+    (residual,) = in_hbm(residual)
     return pl.pallas_call(
-        functools.partial(finish_kernel, first, len(mixed)),
+        functools.partial(finish_kernel, first),
         out_shape=(
             pltpu.HBM((tokens, width), jnp.bfloat16),
             pltpu.HBM(latents.shape, jnp.float32),
             pltpu.HBM(latents.shape, jnp.bfloat16),
         ),
-        in_specs=[SCALARS] * 3
-        + [REMAIN] * 2
-        + [WHOLE] * 3
-        + [REMAIN]
-        + [WHOLE] * len(mixed)
-        + [REMAIN] * len(so_far),
+        in_specs=[WHOLE, REMAIN] + [WHOLE] * 6 + [REMAIN] * len(so_far),
         out_specs=(REMAIN,) * 3,
         scratch_shapes=[
             pltpu.VMEM((count, width), jnp.float32),
-            pltpu.VMEM(weight.shape, jnp.bfloat16),
-            pltpu.VMEM((lines, LANES), jnp.float32),
             pltpu.VMEM((count, width), jnp.bfloat16),
             pltpu.VMEM((lines, LANES), jnp.float32),
             pltpu.VMEM((lines, LANES), jnp.bfloat16),
-            pltpu.VMEM((count, weight.shape[0]), jnp.bfloat16),
-            pltpu.SemaphoreType.DMA((5 + count // QUERY_BLOCK,)),
+            pltpu.SemaphoreType.DMA((2 + 2 * (count // QUERY_BLOCK),)),
         ],
         input_output_aliases={known + place: place for place in range(len(so_far))},
         compiler_params=PARAMS,
         cost_estimate=cost(0.012 * count),
         name="finish",
-    )(level, table, frame, residual, weight, modulation, gain, out_weight, latents, *mixed, *so_far)
+    )(delta, residual, mixed, weight, modulation, gain, out_weight, latents, *so_far)
 
 
 FIRST_BLOCKS = 1
@@ -581,8 +621,8 @@
     frame = lax.axis_index("frame").astype(jnp.int32).reshape(1)
     spatial_turned = jnp.transpose(spatial_qkv)
     temporal_turned = jnp.transpose(temporal_qkv)
-    keys, values, normed, modulation, placed = keys_and_values(
-        level_index, time_table, frame_offset, frame, hidden, mod_table[None, :],
+    keys, values, normed, modulation, placed, delta = keys_and_values(
+        level_index, time_table, frame_offset, frame, hidden, mod_table.reshape(-1, LANES),
         time_weight, spatial_turned, head_count,
     )
     swap = [(0, 1), (1, 0)]
@@ -605,13 +645,12 @@
     last = residuals[-1]
     returned = []
     for parts in gathered:
-        mixed = mix_frames(parts, temporal_turned, attended, (last,))
-        returned.append(exchange(mixed, peers))
+        mixed = mix_frames(frame, parts, temporal_turned, attended, (last,))
+        returned.append(exchange([mixed], peers)[0])
     so_far = ()
     for (first, _), residual, mixed in zip(chunks, residuals, returned):
-        mixed = [part.reshape(-1, attended) for part in mixed]
         so_far = finish(
-            first, so_far, level_index, time_table, frame, residual, mixed, temporal_out,
+            first, so_far, delta, residual, mixed.reshape(-1, attended), temporal_out,
             modulation, final_gain[None, :], jnp.transpose(out_weight), latents[0], tokens,
         )
     hidden_out, velocity, update = so_far

time: 123 us -> 112 us (0.911); the launches traced: 121 us -> 111 us
  Pallas kernels: 59.8 us -> 48.2 us
  waiting for transfers between devices: 10.2 us -> 18 us
  starting transfers between devices: 46.7 us -> 41.5 us
    ppermute x14 -> x7, starting transfers between devices: 30.2 us -> 12.1 us  [exchange(): arrived.append(lax.ppermute(parts[slot], 'frame', pairs))]
    all_to_all x2 -> x3, starting transfers between devices: 12.5 us -> 25.4 us  [exchange(): return [lax.all_to_all(parts[0], 'frame', 0, 0, tiled=True)]]
    all_to_all x2 -> x3, waiting for transfers between devices: 0.01 us -> 10.3 us  [exchange(): return [lax.all_to_all(parts[0], 'frame', 0, 0, tiled=True)]]
    pallas_call x2, Pallas kernels: 23.8 us -> 16.5 us  [attend(): pl.pallas_call(functools.partial(attend_kernel, first, resident, slots),...]
    pallas_call x2, Pallas kernels: 10 us -> 7.29 us  [finish(): pl.pallas_call(functools.partial(finish_kernel, first), out_shape=(pltpu....]
    ppermute x14 -> x7, waiting for transfers between devices: 7.04 us -> 4.57 us  [exchange(): arrived.append(lax.ppermute(parts[slot], 'frame', pairs))]
  transfers between devices with their start and end apart: 19 -> 13, of which waited for: 5 -> 5; matrix products, arithmetic and copies ran while one was open for 0% -> 0% of each run, Pallas kernels for 33% -> 30%
where the time goes in v2:
time: 112 us; the launch traced here: 111 us
  Pallas kernels  48.2 us (43%)
  starting transfers between devices  41.5 us (37%)
  waiting for transfers between devices  18 us (16%)
  between operations  2.13 us (2%)
    all_to_all x3, starting transfers between devices, exchange(): return [lax.all_to_all(parts[0], 'frame', 0, 0, tiled=True)]  25.4 us
    pallas_call x2, Pallas kernels, attend(): pl.pallas_call(functools.partial(attend_kernel, first, resident, slots),...  16.5 us
    pallas_call x2, Pallas kernels, mix_frames(): pl.pallas_call(functools.partial(temporal_kernel, group, tokens, parts),...  16.2 us
    ppermute x7, starting transfers between devices, exchange(): arrived.append(lax.ppermute(parts[slot], 'frame', pairs))  12.1 us
    all_to_all x3, waiting for transfers between devices, exchange(): return [lax.all_to_all(parts[0], 'frame', 0, 0, tiled=True)]  10.3 us
    pallas_call x2, Pallas kernels, finish(): pl.pallas_call(functools.partial(finish_kernel, first), out_shape=(pltpu....  7.29 us
    pallas_call x1, Pallas kernels, keys_and_values(): pl.pallas_call(keys_values_kernel, out_shape=(jax.ShapeDtypeStruct((head_...  5.29 us
    ppermute x7, waiting for transfers between devices, exchange(): arrived.append(lax.ppermute(parts[slot], 'frame', pairs))  4.57 us
  transfers between devices with their start and end apart: 13, of which 5 were waited for; matrix products, arithmetic and copies ran while one was open for 0% of the time, Pallas kernels for 30%

profile of v2, /device:TPU:0, one launch (start us, length us, event | category | flops | bytes accessed | tf_op | source)
XLA Modules:
  0.0 111.5 jit_solution(8665276112675339317)
XLA Ops:
  1.9 5.3 %keys_and_values.1 = (bf16[8,768,128]{2,1,0:T(8,128)(2,1)S(1)}, bf16[8,80,768]{2,1,0:T(8,128)(2,1)S(1)}, bf16[768,1152]{1,0:T(8,128)(2,1)S(1)}, f32[1,3456]{1,0:...) custom-call(s32[1]{0:T(128)S(6)} %copy.23.level, s32[1]{0:T(128)S(6)} %copy.24.offset, s32[1]{0:T(128)} %bitcast.frame, ...), custom_call_target="tpu_custom_call" | custom-call | flops 5000000000 | bytes 1048576 | tf_op jit(solution)/shard_map/keys_and_values/pallas_call | solution.py:154
  7.2 0.0 copy-start
  7.2 0.0 copy-start.3
  7.2 0.6 collective-permute-start
  7.8 0.1 collective-permute-start.1
  7.9 2.9 %project_queries.1.queries_in = bf16[8,128,768]{2,1,0:T(8,128)(2,1)S(1)} custom-call(bf16[768,1152]{1,0:T(8,128)(2,1)S(1)} %get-tuple-element.27.normed, bf16[1728,1152]{1,0:T(8,128)(2,1)} %bitcast.31), custom_call_target="tpu_custom_call" | custom-call | flops 3000000000 | bytes 1048576 | tf_op jit(solution)/shard_map/project_queries/pallas_call | solution.py:198
  10.8 0.0 copy-start.8
  10.8 1.4 %collective-permute-done.1.other_values_in = bf16[8,80,768]{2,1,0:T(8,128)(2,1)S(1)} collective-permute-done((bf16[8,80,768]{2,1,0:T(8,128)(2,1)S(1)}, bf16[8,80,768]{2,1,0:T(8,128)(2,1)S(1)}, u32[]{:S(2)}, u32[]{:S(2)}) %collective-permute-start.1) | collective-permute-done | bytes 983072 | tf_op jit(solution)/shard_map/ppermute | solution.py:629
  12.2 0.0 copy-start.4
  12.2 0.0 collective-permute-done.other_keys_in
  12.3 0.0 copy-start.1
  12.3 0.0 copy-done
  12.3 0.0 copy-done.3
  12.3 5.7 %attend.3 = (f32[256,1152]{1,0:T(8,128)}, bf16[256,1152]{1,0:T(8,128)(2,1)}) custom-call(s32[1]{0:T(128)} %bitcast.frame, bf16[768,1152]{1,0:T(8,128)(2,1)} %bitcast.35, bf16[8,128,768]{2,1,0:T(8,128)(2,1)S(1)} %project_queries.1.queries_in, bf16[8,768,128]{2,1,0:T(8,128)(2,1)S(1)} %get-tuple-element.28.keys_in, ...), custom_call_target="tpu_custom_call" | custom-call | flops 7168000000 | bytes 1048576 | tf_op jit(solution)/shard_map/attend/pallas_call | solution.py:369
  17.9 0.0 copy-done.8
  18.0 0.0 copy-done.4
  18.0 0.0 copy-done.1
  18.0 7.2 %all-to-all-start.1 = ((bf16[8,32,1152]{2,1,0:T(8,128)(2,1)}), bf16[8,32,1152]{2,1,0:T(8,128)(2,1)S(1)}, u32[]{:S(2)}, u32[]{:S(2)}) async-start(bf16[8,32,1152]{2,1,0:T(8,128)(2,1)} %bitcast.29), calls=%async_computation.1 | async-start | bytes 1179648 | tf_op jit(solution)/shard_map/all_to_all | solution.py:592
  25.2 10.8 %attend.2 = (f32[512,1152]{1,0:T(8,128)}, bf16[64,1152]{1,0:T(8,128)(2,1)}, bf16[64,1152]{1,0:T(8,128)(2,1)}, bf16[64,1152]{1,0:T(8,128)(2,1)}, bf16[64,1152]{1,...) custom-call(s32[1]{0:T(128)} %bitcast.frame, ...), custom_call_target="tpu_custom_call" | custom-call | flops 14336000000 | bytes 1048576 | tf_op jit(solution)/shard_map/attend/pallas_call | solution.py:369
  36.0 2.1 %collective-permute-start.2 = (bf16[1,64,1152]{2,1,0:T(8,128)(2,1)}, bf16[1,64,1152]{2,1,0:T(8,128)(2,1)S(1)}, u32[]{:S(2)}, u32[]{:S(2)}) collective-permute-start(bf16[1,64,1152]{2,1,0:T(8,128)(2,1)} %bitcast.43), channel_id=1, source_target_pairs={{0,2},{2,0},{4,6},{6,4},{8,10},{10,8},{12,14},{14,12},{1,3},{3,1},... | collective-permute-start | bytes 442376 | tf_op jit(solution)/shard_map/ppermute | solution.py:596
  38.1 1.5 %collective-permute-start.3 = (bf16[1,64,1152]{2,1,0:T(8,128)(2,1)}, bf16[1,64,1152]{2,1,0:T(8,128)(2,1)S(1)}, u32[]{:S(2)}, u32[]{:S(2)}) collective-permute-start(bf16[1,64,1152]{2,1,0:T(8,128)(2,1)} %bitcast.42), channel_id=1, source_target_pairs={{0,4},{2,6},{4,0},{6,2},{8,12},{10,14},{12,8},{14,10},{1,5},{3,7},... | collective-permute-start | bytes 442376 | tf_op jit(solution)/shard_map/ppermute | solution.py:596
  39.6 0.1 collective-permute-start.4
  39.7 2.9 %collective-permute-start.5 = (bf16[1,64,1152]{2,1,0:T(8,128)(2,1)}, bf16[1,64,1152]{2,1,0:T(8,128)(2,1)S(1)}, u32[]{:S(2)}, u32[]{:S(2)}) collective-permute-start(bf16[1,64,1152]{2,1,0:T(8,128)(2,1)} %bitcast.40), channel_id=1, source_target_pairs={{0,8},{2,10},{4,12},{6,14},{8,0},{10,2},{12,4},{14,6},{1,9},{3,11}... | collective-permute-start | bytes 442376 | tf_op jit(solution)/shard_map/ppermute | solution.py:596
  42.5 1.4 %collective-permute-start.6 = (bf16[1,64,1152]{2,1,0:T(8,128)(2,1)}, bf16[1,64,1152]{2,1,0:T(8,128)(2,1)S(1)}, u32[]{:S(2)}, u32[]{:S(2)}) collective-permute-start(bf16[1,64,1152]{2,1,0:T(8,128)(2,1)} %bitcast.39), channel_id=1, source_target_pairs={{0,10},{2,8},{4,14},{6,12},{8,2},{10,0},{12,6},{14,4},{1,11},{3,9}... | collective-permute-start | bytes 442376 | tf_op jit(solution)/shard_map/ppermute | solution.py:596
  44.0 0.0 collective-permute-done.2.refs_1_
  44.0 3.3 %collective-permute-start.7 = (bf16[1,64,1152]{2,1,0:T(8,128)(2,1)}, bf16[1,64,1152]{2,1,0:T(8,128)(2,1)S(1)}, u32[]{:S(2)}, u32[]{:S(2)}) collective-permute-start(bf16[1,64,1152]{2,1,0:T(8,128)(2,1)} %bitcast.38), channel_id=1, source_target_pairs={{0,12},{2,14},{4,8},{6,10},{8,4},{10,6},{12,0},{14,2},{1,13},{3,15... | collective-permute-start | bytes 442376 | tf_op jit(solution)/shard_map/ppermute | solution.py:596
  47.2 3.1 %collective-permute-done.3.refs_2_ = bf16[1,64,1152]{2,1,0:T(8,128)(2,1)S(1)} collective-permute-done((bf16[1,64,1152]{2,1,0:T(8,128)(2,1)}, bf16[1,64,1152]{2,1,0:T(8,128)(2,1)S(1)}, u32[]{:S(2)}, u32[]{:S(2)}) %collective-permute-start.3) | collective-permute-done | bytes 147488 | tf_op jit(solution)/shard_map/ppermute | solution.py:596
  50.3 0.9 collective-permute-start.8
  51.2 0.0 all-to-all-done.1.refs_0_
  51.2 6.8 %mix_frames.3 = bf16[8,32,576]{2,1,0:T(8,128)(2,1)} custom-call(s32[1]{0:T(128)} %bitcast.frame, bf16[8,32,1152]{2,1,0:T(8,128)(2,1)S(1)} %all-to-all-done.1.refs_0_, bf16[1728,1152]{1,0:T(8,128)(2,1)} %bitcast.32, f32[512,1152]{1,0:T(8,128)} %get-tuple-element.32.refs_9_.refs_2_.residual_far), custom_call_target="tpu_custom_call" | custom-call | flops 6400000000 | bytes 1048576 | tf_op jit(solution)/shard_map/mix_frames/pallas_call | solution.py:468
  58.1 5.1 %all-to-all-start.2 = ((bf16[8,32,576]{2,1,0:T(8,128)(2,1)}), bf16[8,32,576]{2,1,0:T(8,128)(2,1)S(1)}, u32[]{:S(2)}, u32[]{:S(2)}) async-start(bf16[8,32,576]{2,1,0:T(8,128)(2,1)} %mix_frames.3), calls=%async_computation.2 | async-start | bytes 655360 | tf_op jit(solution)/shard_map/all_to_all | solution.py:592
  63.2 0.0 collective-permute-done.4.refs_3_
  63.2 0.0 collective-permute-done.5.refs_4_
  63.2 1.5 %collective-permute-done.6.refs_5_ = bf16[1,64,1152]{2,1,0:T(8,128)(2,1)S(1)} collective-permute-done((bf16[1,64,1152]{2,1,0:T(8,128)(2,1)}, bf16[1,64,1152]{2,1,0:T(8,128)(2,1)S(1)}, u32[]{:S(2)}, u32[]{:S(2)}) %collective-permute-start.6) | collective-permute-done | bytes 147488 | tf_op jit(solution)/shard_map/ppermute | solution.py:596
  64.7 0.0 collective-permute-done.7.refs_6_
  64.7 0.0 collective-permute-done.8.refs_7_
  64.7 0.0 copy-start.7
  64.7 0.9 copy-done.7
  65.6 0.0 copy-start.10
  65.6 0.0 copy-start.2
  65.6 0.0 copy-start.5
  65.6 0.0 copy-start.6
  65.6 9.4 %mix_frames.2 = bf16[8,64,576]{2,1,0:T(8,128)(2,1)} custom-call(s32[1]{0:T(128)} %bitcast.frame, bf16[1,64,1152]{2,1,0:T(8,128)(2,1)S(1)} %bitcast.28, bf16[1,64,1152]{2,1,0:T(8,128)(2,1)S(1)} %collective-permute-done.2.refs_1_, bf16[1,64,1152]{2,1,0:T(8,128)(2,1)S(1)} %collective-permute-done.3.refs_2_, ...), custom_call_target="tpu_custom_call" | custom-call | flops 6400000000 | bytes 1048576 | tf_op jit(solution)/shard_map/mix_frames/pallas_call | solution.py:468
  75.0 0.0 all-to-all-done.2
  75.1 13.0 %all-to-all-start = ((bf16[8,64,576]{2,1,0:T(8,128)(2,1)}), bf16[8,64,576]{2,1,0:T(8,128)(2,1)S(1)}, u32[]{:S(2)}, u32[]{:S(2)}) async-start(bf16[8,64,576]{2,1,0:T(8,128)(2,1)} %mix_frames.2), calls=%async_computation | async-start | bytes 1310720 | tf_op jit(solution)/shard_map/all_to_all | solution.py:592
  88.1 0.0 copy-done.10
  88.1 0.0 copy-done.2
  88.1 0.0 copy-done.5
  88.1 0.0 copy-done.6
  88.1 3.4 %finish.2 = (bf16[768,1152]{1,0:T(8,128)(2,1)}, f32[96,128]{1,0:T(8,128)}, bf16[96,128]{1,0:T(8,128)(2,1)}) custom-call(f32[1,128]{1,0:T(1,128)S(1)} %get-tuple-element.26.delta, f32[256,1152]{1,0:T(8,128)} %get-tuple-element.41.residual_far, bf16[256,576]{1,0:T(8,128)(2,1)S(1)} %bitcast.23, bf16[576,1152]{1,0:T(8,128)(2,1)S(1)} %copy-done.2, ...), custom_call_target="tpu_custom_call" | custom-call | flops 3072000000 | bytes 1048576 | tf_op jit(solution)/shard_map/finish/pallas_call | solution.py:551
  91.6 10.3 %all-to-all-done = bf16[8,64,576]{2,1,0:T(8,128)(2,1)S(1)} async-done(((bf16[8,64,576]{2,1,0:T(8,128)(2,1)}), bf16[8,64,576]{2,1,0:T(8,128)(2,1)S(1)}, u32[]{:S(2)}, u32[]{:S(2)}) %all-to-all-start) | async-done | bytes 589856 | tf_op jit(solution)/shard_map/all_to_all | solution.py:592
  101.8 0.0 copy-start.9
  101.8 3.9 %finish.3 = (bf16[768,1152]{1,0:T(8,128)(2,1)}, f32[96,128]{1,0:T(8,128)}, bf16[96,128]{1,0:T(8,128)(2,1)}) custom-call(f32[1,128]{1,0:T(1,128)S(1)} %get-tuple-element.26.delta, f32[512,1152]{1,0:T(8,128)} %get-tuple-element.32.refs_9_.refs_2_.residual_far, ...), custom_call_target="tpu_custom_call", output_to_operand_aliasing={{0}: (8, {}), {1}: (9, {}), {2}: (10, {})} | custom-call | flops 6144000000 | bytes 1048576 | tf_op jit(solution)/shard_map/finish/pallas_call | solution.py:551
  105.7 3.4 %collective-permute-start.9 = (bf16[96,128]{1,0:T(8,128)(2,1)}, bf16[96,128]{1,0:T(8,128)(2,1)S(1)}, u32[]{:S(2)}, u32[]{:S(2)}) collective-permute-start(bf16[96,128]{1,0:T(8,128)(2,1)} %get-tuple-element.48), channel_id=1, source_target_pairs={{0,2},{2,4},{4,6},{6,8},{8,10},{10,12},{12,14},{1,3},{3,5},{5,7},{... | collective-permute-start | bytes 73736 | tf_op jit(solution)/shard_map/ppermute | solution.py:37
  109.1 1.7 %collective-permute-done.9 = bf16[96,128]{1,0:T(8,128)(2,1)S(1)} collective-permute-done((bf16[96,128]{1,0:T(8,128)(2,1)}, bf16[96,128]{1,0:T(8,128)(2,1)S(1)}, u32[]{:S(2)}, u32[]{:S(2)}) %collective-permute-start.9) | collective-permute-done | bytes 24608 | tf_op jit(solution)/shard_map/ppermute | solution.py:37
  110.8 0.0 copy-done.9
  110.8 0.6 select_bitcast_fusion
  (1 shorter events, 0.0 us)
Async XLA Ops:
  7.2 5.0 %copy-start = (bf16[8,768,128]{2,1,0:T(8,128)(2,1)}, bf16[8,768,128]{2,1,0:T(8,128)(2,1)S(1)}, u32[]{:S(2)}) copy-start(bf16[8,768,128]{2,1,0:T(8,128)(2,1)S(1)} %get-tuple-element.28.keys_in) | copy-start | bytes 4718596
  7.2 5.0 %copy-start.3 = (bf16[8,80,768]{2,1,0:T(8,128)(2,1)}, bf16[8,80,768]{2,1,0:T(8,128)(2,1)S(1)}, u32[]{:S(2)}) copy-start(bf16[8,80,768]{2,1,0:T(8,128)(2,1)S(1)} %get-tuple-element.29.values_in) | copy-start | bytes 2949124
  7.2 5.0 %collective-permute-start = (bf16[8,768,128]{2,1,0:T(8,128)(2,1)S(1)}, bf16[8,768,128]{2,1,0:T(8,128)(2,1)S(1)}, u32[]{:S(2)}, u32[]{:S(2)}) collective-permute-start(bf16[8,768,128]{2,1,0:T(8,128)(2,1)S(1)} %get-tuple-element.28.keys_in), channel_id=1, source_target_pairs={{0,1},{1,0},{2,3},{3,2},{4,5},{5,4},{6,7},{7,6},{8,9},{9,8},{10,11... | collective-permute-start | bytes 4718600 | tf_op jit(solution)/shard_map/ppermute | solution.py:629
  7.8 4.4 %collective-permute-start.1 = (bf16[8,80,768]{2,1,0:T(8,128)(2,1)S(1)}, bf16[8,80,768]{2,1,0:T(8,128)(2,1)S(1)}, u32[]{:S(2)}, u32[]{:S(2)}) collective-permute-start(bf16[8,80,768]{2,1,0:T(8,128)(2,1)S(1)} %get-tuple-element.29.values_in), channel_id=1, source_target_pairs={{0,1},{1,0},{2,3},{3,2},{4,5},{5,4},{6,7},{7,6},{8,9},{9,8},{10,11... | collective-permute-start | bytes 2949128 | tf_op jit(solution)/shard_map/ppermute | solution.py:629
  10.8 7.2 %copy-start.8 = (bf16[8,128,768]{2,1,0:T(8,128)(2,1)}, bf16[8,128,768]{2,1,0:T(8,128)(2,1)S(1)}, u32[]{:S(2)}) copy-start(bf16[8,128,768]{2,1,0:T(8,128)(2,1)S(1)} %project_queries.1.queries_in) | copy-start | bytes 4718596
  12.2 5.7 %copy-start.4 = (bf16[8,80,768]{2,1,0:T(8,128)(2,1)}, bf16[8,80,768]{2,1,0:T(8,128)(2,1)S(1)}, u32[]{:S(2)}) copy-start(bf16[8,80,768]{2,1,0:T(8,128)(2,1)S(1)} %collective-permute-done.1.other_values_in) | copy-start | bytes 2949124
  12.3 5.7 %copy-start.1 = (bf16[8,768,128]{2,1,0:T(8,128)(2,1)}, bf16[8,768,128]{2,1,0:T(8,128)(2,1)S(1)}, u32[]{:S(2)}) copy-start(bf16[8,768,128]{2,1,0:T(8,128)(2,1)S(1)} %collective-permute-done.other_keys_in) | copy-start | bytes 4718596
  18.0 33.2 %all-to-all-start.1 = ((bf16[8,32,1152]{2,1,0:T(8,128)(2,1)}), bf16[8,32,1152]{2,1,0:T(8,128)(2,1)S(1)}, u32[]{:S(2)}, u32[]{:S(2)}) async-start(bf16[8,32,1152]{2,1,0:T(8,128)(2,1)} %bitcast.29), calls=%async_computation.1 | async-start | bytes 1179648 | tf_op jit(solution)/shard_map/all_to_all | solution.py:592
  36.0 7.9 %collective-permute-start.2 = (bf16[1,64,1152]{2,1,0:T(8,128)(2,1)}, bf16[1,64,1152]{2,1,0:T(8,128)(2,1)S(1)}, u32[]{:S(2)}, u32[]{:S(2)}) collective-permute-start(bf16[1,64,1152]{2,1,0:T(8,128)(2,1)} %bitcast.43), channel_id=1, source_target_pairs={{0,2},{2,0},{4,6},{6,4},{8,10},{10,8},{12,14},{14,12},{1,3},{3,1},... | collective-permute-start | bytes 442376 | tf_op jit(solution)/shard_map/ppermute | solution.py:596
  38.1 12.2 %collective-permute-start.3 = (bf16[1,64,1152]{2,1,0:T(8,128)(2,1)}, bf16[1,64,1152]{2,1,0:T(8,128)(2,1)S(1)}, u32[]{:S(2)}, u32[]{:S(2)}) collective-permute-start(bf16[1,64,1152]{2,1,0:T(8,128)(2,1)} %bitcast.42), channel_id=1, source_target_pairs={{0,4},{2,6},{4,0},{6,2},{8,12},{10,14},{12,8},{14,10},{1,5},{3,7},... | collective-permute-start | bytes 442376 | tf_op jit(solution)/shard_map/ppermute | solution.py:596
  39.6 23.6 %collective-permute-start.4 = (bf16[1,64,1152]{2,1,0:T(8,128)(2,1)}, bf16[1,64,1152]{2,1,0:T(8,128)(2,1)S(1)}, u32[]{:S(2)}, u32[]{:S(2)}) collective-permute-start(bf16[1,64,1152]{2,1,0:T(8,128)(2,1)} %bitcast.41), channel_id=1, source_target_pairs={{0,6},{2,4},{4,2},{6,0},{8,14},{10,12},{12,10},{14,8},{1,7},{3,5},... | collective-permute-start | bytes 442376 | tf_op jit(solution)/shard_map/ppermute | solution.py:596
  39.7 23.5 %collective-permute-start.5 = (bf16[1,64,1152]{2,1,0:T(8,128)(2,1)}, bf16[1,64,1152]{2,1,0:T(8,128)(2,1)S(1)}, u32[]{:S(2)}, u32[]{:S(2)}) collective-permute-start(bf16[1,64,1152]{2,1,0:T(8,128)(2,1)} %bitcast.40), channel_id=1, source_target_pairs={{0,8},{2,10},{4,12},{6,14},{8,0},{10,2},{12,4},{14,6},{1,9},{3,11}... | collective-permute-start | bytes 442376 | tf_op jit(solution)/shard_map/ppermute | solution.py:596
  42.5 22.1 %collective-permute-start.6 = (bf16[1,64,1152]{2,1,0:T(8,128)(2,1)}, bf16[1,64,1152]{2,1,0:T(8,128)(2,1)S(1)}, u32[]{:S(2)}, u32[]{:S(2)}) collective-permute-start(bf16[1,64,1152]{2,1,0:T(8,128)(2,1)} %bitcast.39), channel_id=1, source_target_pairs={{0,10},{2,8},{4,14},{6,12},{8,2},{10,0},{12,6},{14,4},{1,11},{3,9}... | collective-permute-start | bytes 442376 | tf_op jit(solution)/shard_map/ppermute | solution.py:596
  44.0 20.7 %collective-permute-start.7 = (bf16[1,64,1152]{2,1,0:T(8,128)(2,1)}, bf16[1,64,1152]{2,1,0:T(8,128)(2,1)S(1)}, u32[]{:S(2)}, u32[]{:S(2)}) collective-permute-start(bf16[1,64,1152]{2,1,0:T(8,128)(2,1)} %bitcast.38), channel_id=1, source_target_pairs={{0,12},{2,14},{4,8},{6,10},{8,4},{10,6},{12,0},{14,2},{1,13},{3,15... | collective-permute-start | bytes 442376 | tf_op jit(solution)/shard_map/ppermute | solution.py:596
  50.3 14.4 %collective-permute-start.8 = (bf16[1,64,1152]{2,1,0:T(8,128)(2,1)}, bf16[1,64,1152]{2,1,0:T(8,128)(2,1)S(1)}, u32[]{:S(2)}, u32[]{:S(2)}) collective-permute-start(bf16[1,64,1152]{2,1,0:T(8,128)(2,1)} %bitcast.37), channel_id=1, source_target_pairs={{0,14},{2,12},{4,10},{6,8},{8,6},{10,4},{12,2},{14,0},{1,15},{3,13... | collective-permute-start | bytes 442376 | tf_op jit(solution)/shard_map/ppermute | solution.py:596
  58.1 17.0 %all-to-all-start.2 = ((bf16[8,32,576]{2,1,0:T(8,128)(2,1)}), bf16[8,32,576]{2,1,0:T(8,128)(2,1)S(1)}, u32[]{:S(2)}, u32[]{:S(2)}) async-start(bf16[8,32,576]{2,1,0:T(8,128)(2,1)} %mix_frames.3), calls=%async_computation.2 | async-start | bytes 655360 | tf_op jit(solution)/shard_map/all_to_all | solution.py:592
  64.7 0.9 copy-start.7
  65.6 22.5 %copy-start.10 = (f32[1152]{0:T(1024)S(1)}, f32[1152]{0:T(1024)}, u32[]{:S(2)}) copy-start(f32[1152]{0:T(1024)} %param.26) | copy-start | bytes 13828
  65.6 22.5 %copy-start.2 = (bf16[576,1152]{1,0:T(8,128)(2,1)S(1)}, bf16[576,1152]{1,0:T(8,128)(2,1)}, u32[]{:S(2)}) copy-start(bf16[576,1152]{1,0:T(8,128)(2,1)} %weight.3) | copy-start | bytes 3981316
  65.6 22.5 %copy-start.5 = (f32[1,96,128]{2,1,0:T(8,128)S(1)}, f32[1,96,128]{2,1,0:T(8,128)}, u32[]{:S(2)}) copy-start(f32[1,96,128]{2,1,0:T(8,128)} %param.15) | copy-start | bytes 147460
  65.6 22.5 %copy-start.6 = (bf16[1152,16]{0,1:T(8,128)(2,1)S(1)}, bf16[1152,16]{0,1:T(8,128)(2,1)}, u32[]{:S(2)}) copy-start(bf16[1152,16]{0,1:T(8,128)(2,1)} %param.27) | copy-start | bytes 110596
  75.1 26.8 %all-to-all-start = ((bf16[8,64,576]{2,1,0:T(8,128)(2,1)}), bf16[8,64,576]{2,1,0:T(8,128)(2,1)S(1)}, u32[]{:S(2)}, u32[]{:S(2)}) async-start(bf16[8,64,576]{2,1,0:T(8,128)(2,1)} %mix_frames.2), calls=%async_computation | async-start | bytes 1310720 | tf_op jit(solution)/shard_map/all_to_all | solution.py:592
  101.8 9.0 %copy-start.9 = (f32[96,128]{1,0:T(8,128)S(1)}, f32[96,128]{1,0:T(8,128)}, u32[]{:S(2)}) copy-start(f32[96,128]{1,0:T(8,128)} %param.16) | copy-start | bytes 147460
  105.7 5.1 %collective-permute-start.9 = (bf16[96,128]{1,0:T(8,128)(2,1)}, bf16[96,128]{1,0:T(8,128)(2,1)S(1)}, u32[]{:S(2)}, u32[]{:S(2)}) collective-permute-start(bf16[96,128]{1,0:T(8,128)(2,1)} %get-tuple-element.48), channel_id=1, source_target_pairs={{0,2},{2,4},{4,6},{6,8},{8,10},{10,12},{12,14},{1,3},{3,5},{5,7},{... | collective-permute-start | bytes 73736 | tf_op jit(solution)/shard_map/ppermute | solution.py:37

commit v3 on v2

--- a/solution.py
+++ b/solution.py
@@ -590,10 +590,10 @@
 def exchange(parts, peers):
     if len(parts) == 1:
         return [lax.all_to_all(parts[0], "frame", 0, 0, tiled=True)]
-    arrived = [parts[0]]
-    for slot in range(1, peers):
+    arrived = list(parts)
+    for slot in reversed(range(1, peers)):
         pairs = [(index, index ^ slot) for index in range(peers)]
-        arrived.append(lax.ppermute(parts[slot], "frame", pairs))
+        arrived[slot] = lax.ppermute(parts[slot], "frame", pairs)
     return arrived
 
 

time: 112 us -> 112 us (level)
  no operation moved by 1% of the time
where the time goes in v3:
time: 112 us; the launch traced here: 111 us
  Pallas kernels  48.2 us (43%)
  starting transfers between devices  41.5 us (37%)
  waiting for transfers between devices  18 us (16%)
  between operations  2.13 us (2%)
    all_to_all x3, starting transfers between devices, exchange(): return [lax.all_to_all(parts[0], 'frame', 0, 0, tiled=True)]  25.4 us
    pallas_call x2, Pallas kernels, attend(): pl.pallas_call(functools.partial(attend_kernel, first, resident, slots),...  16.5 us
    pallas_call x2, Pallas kernels, mix_frames(): pl.pallas_call(functools.partial(temporal_kernel, group, tokens, parts),...  16.2 us
    ppermute x7, starting transfers between devices, exchange(): arrived[slot] = lax.ppermute(parts[slot], 'frame', pairs)  12.1 us
    all_to_all x3, waiting for transfers between devices, exchange(): return [lax.all_to_all(parts[0], 'frame', 0, 0, tiled=True)]  10.3 us
    pallas_call x2, Pallas kernels, finish(): pl.pallas_call(functools.partial(finish_kernel, first), out_shape=(pltpu....  7.29 us
    pallas_call x1, Pallas kernels, keys_and_values(): pl.pallas_call(keys_values_kernel, out_shape=(jax.ShapeDtypeStruct((head_...  5.29 us
    ppermute x7, waiting for transfers between devices, exchange(): arrived[slot] = lax.ppermute(parts[slot], 'frame', pairs)  4.57 us
  transfers between devices with their start and end apart: 13, of which 5 were waited for; matrix products, arithmetic and copies ran while one was open for 0% of the time, Pallas kernels for 30%

profile of v3, /device:TPU:0, one launch (start us, length us, event | category | flops | bytes accessed | tf_op | source)
XLA Modules:
  0.0 111.5 jit_solution(8665276112675339317)
XLA Ops:
  1.9 5.3 %keys_and_values.1 = (bf16[8,768,128]{2,1,0:T(8,128)(2,1)S(1)}, bf16[8,80,768]{2,1,0:T(8,128)(2,1)S(1)}, bf16[768,1152]{1,0:T(8,128)(2,1)S(1)}, f32[1,3456]{1,0:...) custom-call(s32[1]{0:T(128)S(6)} %copy.23.level, s32[1]{0:T(128)S(6)} %copy.24.offset, s32[1]{0:T(128)} %bitcast.frame, ...), custom_call_target="tpu_custom_call" | custom-call | flops 5000000000 | bytes 1048576 | tf_op jit(solution)/shard_map/keys_and_values/pallas_call | solution.py:154
  7.2 0.0 copy-start
  7.2 0.0 copy-start.3
  7.2 0.6 collective-permute-start
  7.8 0.1 collective-permute-start.1
  7.9 2.9 %project_queries.1.queries_in = bf16[8,128,768]{2,1,0:T(8,128)(2,1)S(1)} custom-call(bf16[768,1152]{1,0:T(8,128)(2,1)S(1)} %get-tuple-element.27.normed, bf16[1728,1152]{1,0:T(8,128)(2,1)} %bitcast.31), custom_call_target="tpu_custom_call" | custom-call | flops 3000000000 | bytes 1048576 | tf_op jit(solution)/shard_map/project_queries/pallas_call | solution.py:198
  10.8 0.0 copy-start.8
  10.8 1.4 %collective-permute-done.1.other_values_in = bf16[8,80,768]{2,1,0:T(8,128)(2,1)S(1)} collective-permute-done((bf16[8,80,768]{2,1,0:T(8,128)(2,1)S(1)}, bf16[8,80,768]{2,1,0:T(8,128)(2,1)S(1)}, u32[]{:S(2)}, u32[]{:S(2)}) %collective-permute-start.1) | collective-permute-done | bytes 983072 | tf_op jit(solution)/shard_map/ppermute | solution.py:629
  12.2 0.0 copy-start.4
  12.2 0.0 collective-permute-done.other_keys_in
  12.3 0.0 copy-start.1
  12.3 0.0 copy-done
  12.3 0.0 copy-done.3
  12.3 5.7 %attend.3 = (f32[256,1152]{1,0:T(8,128)}, bf16[256,1152]{1,0:T(8,128)(2,1)}) custom-call(s32[1]{0:T(128)} %bitcast.frame, bf16[768,1152]{1,0:T(8,128)(2,1)} %bitcast.35, bf16[8,128,768]{2,1,0:T(8,128)(2,1)S(1)} %project_queries.1.queries_in, bf16[8,768,128]{2,1,0:T(8,128)(2,1)S(1)} %get-tuple-element.28.keys_in, ...), custom_call_target="tpu_custom_call" | custom-call | flops 7168000000 | bytes 1048576 | tf_op jit(solution)/shard_map/attend/pallas_call | solution.py:369
  17.9 0.0 copy-done.8
  18.0 0.0 copy-done.4
  18.0 0.0 copy-done.1
  18.0 7.2 %all-to-all-start.1 = ((bf16[8,32,1152]{2,1,0:T(8,128)(2,1)}), bf16[8,32,1152]{2,1,0:T(8,128)(2,1)S(1)}, u32[]{:S(2)}, u32[]{:S(2)}) async-start(bf16[8,32,1152]{2,1,0:T(8,128)(2,1)} %bitcast.29), calls=%async_computation.1 | async-start | bytes 1179648 | tf_op jit(solution)/shard_map/all_to_all | solution.py:592
  25.2 10.8 %attend.2 = (f32[512,1152]{1,0:T(8,128)}, bf16[64,1152]{1,0:T(8,128)(2,1)}, bf16[64,1152]{1,0:T(8,128)(2,1)}, bf16[64,1152]{1,0:T(8,128)(2,1)}, bf16[64,1152]{1,...) custom-call(s32[1]{0:T(128)} %bitcast.frame, ...), custom_call_target="tpu_custom_call" | custom-call | flops 14336000000 | bytes 1048576 | tf_op jit(solution)/shard_map/attend/pallas_call | solution.py:369
  36.0 2.1 %collective-permute-start.2 = (bf16[1,64,1152]{2,1,0:T(8,128)(2,1)}, bf16[1,64,1152]{2,1,0:T(8,128)(2,1)S(1)}, u32[]{:S(2)}, u32[]{:S(2)}) collective-permute-start(bf16[1,64,1152]{2,1,0:T(8,128)(2,1)} %bitcast.43), channel_id=1, source_target_pairs={{0,2},{2,0},{4,6},{6,4},{8,10},{10,8},{12,14},{14,12},{1,3},{3,1},... | collective-permute-start | bytes 442376 | tf_op jit(solution)/shard_map/ppermute | solution.py:596
  38.1 1.5 %collective-permute-start.3 = (bf16[1,64,1152]{2,1,0:T(8,128)(2,1)}, bf16[1,64,1152]{2,1,0:T(8,128)(2,1)S(1)}, u32[]{:S(2)}, u32[]{:S(2)}) collective-permute-start(bf16[1,64,1152]{2,1,0:T(8,128)(2,1)} %bitcast.42), channel_id=1, source_target_pairs={{0,4},{2,6},{4,0},{6,2},{8,12},{10,14},{12,8},{14,10},{1,5},{3,7},... | collective-permute-start | bytes 442376 | tf_op jit(solution)/shard_map/ppermute | solution.py:596
  39.6 0.1 collective-permute-start.4
  39.7 2.9 %collective-permute-start.5 = (bf16[1,64,1152]{2,1,0:T(8,128)(2,1)}, bf16[1,64,1152]{2,1,0:T(8,128)(2,1)S(1)}, u32[]{:S(2)}, u32[]{:S(2)}) collective-permute-start(bf16[1,64,1152]{2,1,0:T(8,128)(2,1)} %bitcast.40), channel_id=1, source_target_pairs={{0,8},{2,10},{4,12},{6,14},{8,0},{10,2},{12,4},{14,6},{1,9},{3,11}... | collective-permute-start | bytes 442376 | tf_op jit(solution)/shard_map/ppermute | solution.py:596
  42.5 1.4 %collective-permute-start.6 = (bf16[1,64,1152]{2,1,0:T(8,128)(2,1)}, bf16[1,64,1152]{2,1,0:T(8,128)(2,1)S(1)}, u32[]{:S(2)}, u32[]{:S(2)}) collective-permute-start(bf16[1,64,1152]{2,1,0:T(8,128)(2,1)} %bitcast.39), channel_id=1, source_target_pairs={{0,10},{2,8},{4,14},{6,12},{8,2},{10,0},{12,6},{14,4},{1,11},{3,9}... | collective-permute-start | bytes 442376 | tf_op jit(solution)/shard_map/ppermute | solution.py:596
  44.0 0.0 collective-permute-done.2.refs_1_
  44.0 3.3 %collective-permute-start.7 = (bf16[1,64,1152]{2,1,0:T(8,128)(2,1)}, bf16[1,64,1152]{2,1,0:T(8,128)(2,1)S(1)}, u32[]{:S(2)}, u32[]{:S(2)}) collective-permute-start(bf16[1,64,1152]{2,1,0:T(8,128)(2,1)} %bitcast.38), channel_id=1, source_target_pairs={{0,12},{2,14},{4,8},{6,10},{8,4},{10,6},{12,0},{14,2},{1,13},{3,15... | collective-permute-start | bytes 442376 | tf_op jit(solution)/shard_map/ppermute | solution.py:596
  47.2 3.1 %collective-permute-done.3.refs_2_ = bf16[1,64,1152]{2,1,0:T(8,128)(2,1)S(1)} collective-permute-done((bf16[1,64,1152]{2,1,0:T(8,128)(2,1)}, bf16[1,64,1152]{2,1,0:T(8,128)(2,1)S(1)}, u32[]{:S(2)}, u32[]{:S(2)}) %collective-permute-start.3) | collective-permute-done | bytes 147488 | tf_op jit(solution)/shard_map/ppermute | solution.py:596
  50.3 0.9 collective-permute-start.8
  51.2 0.0 all-to-all-done.1.refs_0_
  51.2 6.8 %mix_frames.3 = bf16[8,32,576]{2,1,0:T(8,128)(2,1)} custom-call(s32[1]{0:T(128)} %bitcast.frame, bf16[8,32,1152]{2,1,0:T(8,128)(2,1)S(1)} %all-to-all-done.1.refs_0_, bf16[1728,1152]{1,0:T(8,128)(2,1)} %bitcast.32, f32[512,1152]{1,0:T(8,128)} %get-tuple-element.32.refs_9_.refs_2_.residual_far), custom_call_target="tpu_custom_call" | custom-call | flops 6400000000 | bytes 1048576 | tf_op jit(solution)/shard_map/mix_frames/pallas_call | solution.py:468
  58.1 5.1 %all-to-all-start.2 = ((bf16[8,32,576]{2,1,0:T(8,128)(2,1)}), bf16[8,32,576]{2,1,0:T(8,128)(2,1)S(1)}, u32[]{:S(2)}, u32[]{:S(2)}) async-start(bf16[8,32,576]{2,1,0:T(8,128)(2,1)} %mix_frames.3), calls=%async_computation.2 | async-start | bytes 655360 | tf_op jit(solution)/shard_map/all_to_all | solution.py:592
  63.2 0.0 collective-permute-done.4.refs_3_
  63.2 0.0 collective-permute-done.5.refs_4_
  63.2 1.5 %collective-permute-done.6.refs_5_ = bf16[1,64,1152]{2,1,0:T(8,128)(2,1)S(1)} collective-permute-done((bf16[1,64,1152]{2,1,0:T(8,128)(2,1)}, bf16[1,64,1152]{2,1,0:T(8,128)(2,1)S(1)}, u32[]{:S(2)}, u32[]{:S(2)}) %collective-permute-start.6) | collective-permute-done | bytes 147488 | tf_op jit(solution)/shard_map/ppermute | solution.py:596
  64.7 0.0 collective-permute-done.7.refs_6_
  64.7 0.0 collective-permute-done.8.refs_7_
  64.7 0.0 copy-start.7
  64.7 0.9 copy-done.7
  65.6 0.0 copy-start.10
  65.6 0.0 copy-start.2
  65.6 0.0 copy-start.5
  65.6 0.0 copy-start.6
  65.6 9.4 %mix_frames.2 = bf16[8,64,576]{2,1,0:T(8,128)(2,1)} custom-call(s32[1]{0:T(128)} %bitcast.frame, bf16[1,64,1152]{2,1,0:T(8,128)(2,1)S(1)} %bitcast.28, bf16[1,64,1152]{2,1,0:T(8,128)(2,1)S(1)} %collective-permute-done.2.refs_1_, bf16[1,64,1152]{2,1,0:T(8,128)(2,1)S(1)} %collective-permute-done.3.refs_2_, ...), custom_call_target="tpu_custom_call" | custom-call | flops 6400000000 | bytes 1048576 | tf_op jit(solution)/shard_map/mix_frames/pallas_call | solution.py:468
  75.0 0.0 all-to-all-done.2
  75.1 13.0 %all-to-all-start = ((bf16[8,64,576]{2,1,0:T(8,128)(2,1)}), bf16[8,64,576]{2,1,0:T(8,128)(2,1)S(1)}, u32[]{:S(2)}, u32[]{:S(2)}) async-start(bf16[8,64,576]{2,1,0:T(8,128)(2,1)} %mix_frames.2), calls=%async_computation | async-start | bytes 1310720 | tf_op jit(solution)/shard_map/all_to_all | solution.py:592
  88.1 0.0 copy-done.10
  88.1 0.0 copy-done.2
  88.1 0.0 copy-done.5
  88.1 0.0 copy-done.6
  88.1 3.4 %finish.2 = (bf16[768,1152]{1,0:T(8,128)(2,1)}, f32[96,128]{1,0:T(8,128)}, bf16[96,128]{1,0:T(8,128)(2,1)}) custom-call(f32[1,128]{1,0:T(1,128)S(1)} %get-tuple-element.26.delta, f32[256,1152]{1,0:T(8,128)} %get-tuple-element.41.residual_far, bf16[256,576]{1,0:T(8,128)(2,1)S(1)} %bitcast.23, bf16[576,1152]{1,0:T(8,128)(2,1)S(1)} %copy-done.2, ...), custom_call_target="tpu_custom_call" | custom-call | flops 3072000000 | bytes 1048576 | tf_op jit(solution)/shard_map/finish/pallas_call | solution.py:551
  91.6 10.3 %all-to-all-done = bf16[8,64,576]{2,1,0:T(8,128)(2,1)S(1)} async-done(((bf16[8,64,576]{2,1,0:T(8,128)(2,1)}), bf16[8,64,576]{2,1,0:T(8,128)(2,1)S(1)}, u32[]{:S(2)}, u32[]{:S(2)}) %all-to-all-start) | async-done | bytes 589856 | tf_op jit(solution)/shard_map/all_to_all | solution.py:592
  101.8 0.0 copy-start.9
  101.8 3.9 %finish.3 = (bf16[768,1152]{1,0:T(8,128)(2,1)}, f32[96,128]{1,0:T(8,128)}, bf16[96,128]{1,0:T(8,128)(2,1)}) custom-call(f32[1,128]{1,0:T(1,128)S(1)} %get-tuple-element.26.delta, f32[512,1152]{1,0:T(8,128)} %get-tuple-element.32.refs_9_.refs_2_.residual_far, ...), custom_call_target="tpu_custom_call", output_to_operand_aliasing={{0}: (8, {}), {1}: (9, {}), {2}: (10, {})} | custom-call | flops 6144000000 | bytes 1048576 | tf_op jit(solution)/shard_map/finish/pallas_call | solution.py:551
  105.7 3.4 %collective-permute-start.9 = (bf16[96,128]{1,0:T(8,128)(2,1)}, bf16[96,128]{1,0:T(8,128)(2,1)S(1)}, u32[]{:S(2)}, u32[]{:S(2)}) collective-permute-start(bf16[96,128]{1,0:T(8,128)(2,1)} %get-tuple-element.48), channel_id=1, source_target_pairs={{0,2},{2,4},{4,6},{6,8},{8,10},{10,12},{12,14},{1,3},{3,5},{5,7},{... | collective-permute-start | bytes 73736 | tf_op jit(solution)/shard_map/ppermute | solution.py:37
  109.1 1.7 %collective-permute-done.9 = bf16[96,128]{1,0:T(8,128)(2,1)S(1)} collective-permute-done((bf16[96,128]{1,0:T(8,128)(2,1)}, bf16[96,128]{1,0:T(8,128)(2,1)S(1)}, u32[]{:S(2)}, u32[]{:S(2)}) %collective-permute-start.9) | collective-permute-done | bytes 24608 | tf_op jit(solution)/shard_map/ppermute | solution.py:37
  110.8 0.0 copy-done.9
  110.8 0.6 select_bitcast_fusion
  (1 shorter events, 0.0 us)
Async XLA Ops:
  7.2 5.0 %copy-start = (bf16[8,768,128]{2,1,0:T(8,128)(2,1)}, bf16[8,768,128]{2,1,0:T(8,128)(2,1)S(1)}, u32[]{:S(2)}) copy-start(bf16[8,768,128]{2,1,0:T(8,128)(2,1)S(1)} %get-tuple-element.28.keys_in) | copy-start | bytes 4718596
  7.2 5.0 %copy-start.3 = (bf16[8,80,768]{2,1,0:T(8,128)(2,1)}, bf16[8,80,768]{2,1,0:T(8,128)(2,1)S(1)}, u32[]{:S(2)}) copy-start(bf16[8,80,768]{2,1,0:T(8,128)(2,1)S(1)} %get-tuple-element.29.values_in) | copy-start | bytes 2949124
  7.2 5.0 %collective-permute-start = (bf16[8,768,128]{2,1,0:T(8,128)(2,1)S(1)}, bf16[8,768,128]{2,1,0:T(8,128)(2,1)S(1)}, u32[]{:S(2)}, u32[]{:S(2)}) collective-permute-start(bf16[8,768,128]{2,1,0:T(8,128)(2,1)S(1)} %get-tuple-element.28.keys_in), channel_id=1, source_target_pairs={{0,1},{1,0},{2,3},{3,2},{4,5},{5,4},{6,7},{7,6},{8,9},{9,8},{10,11... | collective-permute-start | bytes 4718600 | tf_op jit(solution)/shard_map/ppermute | solution.py:629
  7.8 4.4 %collective-permute-start.1 = (bf16[8,80,768]{2,1,0:T(8,128)(2,1)S(1)}, bf16[8,80,768]{2,1,0:T(8,128)(2,1)S(1)}, u32[]{:S(2)}, u32[]{:S(2)}) collective-permute-start(bf16[8,80,768]{2,1,0:T(8,128)(2,1)S(1)} %get-tuple-element.29.values_in), channel_id=1, source_target_pairs={{0,1},{1,0},{2,3},{3,2},{4,5},{5,4},{6,7},{7,6},{8,9},{9,8},{10,11... | collective-permute-start | bytes 2949128 | tf_op jit(solution)/shard_map/ppermute | solution.py:629
  10.8 7.2 %copy-start.8 = (bf16[8,128,768]{2,1,0:T(8,128)(2,1)}, bf16[8,128,768]{2,1,0:T(8,128)(2,1)S(1)}, u32[]{:S(2)}) copy-start(bf16[8,128,768]{2,1,0:T(8,128)(2,1)S(1)} %project_queries.1.queries_in) | copy-start | bytes 4718596
  12.2 5.7 %copy-start.4 = (bf16[8,80,768]{2,1,0:T(8,128)(2,1)}, bf16[8,80,768]{2,1,0:T(8,128)(2,1)S(1)}, u32[]{:S(2)}) copy-start(bf16[8,80,768]{2,1,0:T(8,128)(2,1)S(1)} %collective-permute-done.1.other_values_in) | copy-start | bytes 2949124
  12.3 5.7 %copy-start.1 = (bf16[8,768,128]{2,1,0:T(8,128)(2,1)}, bf16[8,768,128]{2,1,0:T(8,128)(2,1)S(1)}, u32[]{:S(2)}) copy-start(bf16[8,768,128]{2,1,0:T(8,128)(2,1)S(1)} %collective-permute-done.other_keys_in) | copy-start | bytes 4718596
  18.0 33.2 %all-to-all-start.1 = ((bf16[8,32,1152]{2,1,0:T(8,128)(2,1)}), bf16[8,32,1152]{2,1,0:T(8,128)(2,1)S(1)}, u32[]{:S(2)}, u32[]{:S(2)}) async-start(bf16[8,32,1152]{2,1,0:T(8,128)(2,1)} %bitcast.29), calls=%async_computation.1 | async-start | bytes 1179648 | tf_op jit(solution)/shard_map/all_to_all | solution.py:592
  36.0 7.9 %collective-permute-start.2 = (bf16[1,64,1152]{2,1,0:T(8,128)(2,1)}, bf16[1,64,1152]{2,1,0:T(8,128)(2,1)S(1)}, u32[]{:S(2)}, u32[]{:S(2)}) collective-permute-start(bf16[1,64,1152]{2,1,0:T(8,128)(2,1)} %bitcast.43), channel_id=1, source_target_pairs={{0,2},{2,0},{4,6},{6,4},{8,10},{10,8},{12,14},{14,12},{1,3},{3,1},... | collective-permute-start | bytes 442376 | tf_op jit(solution)/shard_map/ppermute | solution.py:596
  38.1 12.2 %collective-permute-start.3 = (bf16[1,64,1152]{2,1,0:T(8,128)(2,1)}, bf16[1,64,1152]{2,1,0:T(8,128)(2,1)S(1)}, u32[]{:S(2)}, u32[]{:S(2)}) collective-permute-start(bf16[1,64,1152]{2,1,0:T(8,128)(2,1)} %bitcast.42), channel_id=1, source_target_pairs={{0,4},{2,6},{4,0},{6,2},{8,12},{10,14},{12,8},{14,10},{1,5},{3,7},... | collective-permute-start | bytes 442376 | tf_op jit(solution)/shard_map/ppermute | solution.py:596
  39.6 23.6 %collective-permute-start.4 = (bf16[1,64,1152]{2,1,0:T(8,128)(2,1)}, bf16[1,64,1152]{2,1,0:T(8,128)(2,1)S(1)}, u32[]{:S(2)}, u32[]{:S(2)}) collective-permute-start(bf16[1,64,1152]{2,1,0:T(8,128)(2,1)} %bitcast.41), channel_id=1, source_target_pairs={{0,6},{2,4},{4,2},{6,0},{8,14},{10,12},{12,10},{14,8},{1,7},{3,5},... | collective-permute-start | bytes 442376 | tf_op jit(solution)/shard_map/ppermute | solution.py:596
  39.7 23.5 %collective-permute-start.5 = (bf16[1,64,1152]{2,1,0:T(8,128)(2,1)}, bf16[1,64,1152]{2,1,0:T(8,128)(2,1)S(1)}, u32[]{:S(2)}, u32[]{:S(2)}) collective-permute-start(bf16[1,64,1152]{2,1,0:T(8,128)(2,1)} %bitcast.40), channel_id=1, source_target_pairs={{0,8},{2,10},{4,12},{6,14},{8,0},{10,2},{12,4},{14,6},{1,9},{3,11}... | collective-permute-start | bytes 442376 | tf_op jit(solution)/shard_map/ppermute | solution.py:596
  42.5 22.1 %collective-permute-start.6 = (bf16[1,64,1152]{2,1,0:T(8,128)(2,1)}, bf16[1,64,1152]{2,1,0:T(8,128)(2,1)S(1)}, u32[]{:S(2)}, u32[]{:S(2)}) collective-permute-start(bf16[1,64,1152]{2,1,0:T(8,128)(2,1)} %bitcast.39), channel_id=1, source_target_pairs={{0,10},{2,8},{4,14},{6,12},{8,2},{10,0},{12,6},{14,4},{1,11},{3,9}... | collective-permute-start | bytes 442376 | tf_op jit(solution)/shard_map/ppermute | solution.py:596
  44.0 20.7 %collective-permute-start.7 = (bf16[1,64,1152]{2,1,0:T(8,128)(2,1)}, bf16[1,64,1152]{2,1,0:T(8,128)(2,1)S(1)}, u32[]{:S(2)}, u32[]{:S(2)}) collective-permute-start(bf16[1,64,1152]{2,1,0:T(8,128)(2,1)} %bitcast.38), channel_id=1, source_target_pairs={{0,12},{2,14},{4,8},{6,10},{8,4},{10,6},{12,0},{14,2},{1,13},{3,15... | collective-permute-start | bytes 442376 | tf_op jit(solution)/shard_map/ppermute | solution.py:596
  50.3 14.4 %collective-permute-start.8 = (bf16[1,64,1152]{2,1,0:T(8,128)(2,1)}, bf16[1,64,1152]{2,1,0:T(8,128)(2,1)S(1)}, u32[]{:S(2)}, u32[]{:S(2)}) collective-permute-start(bf16[1,64,1152]{2,1,0:T(8,128)(2,1)} %bitcast.37), channel_id=1, source_target_pairs={{0,14},{2,12},{4,10},{6,8},{8,6},{10,4},{12,2},{14,0},{1,15},{3,13... | collective-permute-start | bytes 442376 | tf_op jit(solution)/shard_map/ppermute | solution.py:596
  58.1 17.0 %all-to-all-start.2 = ((bf16[8,32,576]{2,1,0:T(8,128)(2,1)}), bf16[8,32,576]{2,1,0:T(8,128)(2,1)S(1)}, u32[]{:S(2)}, u32[]{:S(2)}) async-start(bf16[8,32,576]{2,1,0:T(8,128)(2,1)} %mix_frames.3), calls=%async_computation.2 | async-start | bytes 655360 | tf_op jit(solution)/shard_map/all_to_all | solution.py:592
  64.7 0.9 copy-start.7
  65.6 22.5 %copy-start.10 = (f32[1152]{0:T(1024)S(1)}, f32[1152]{0:T(1024)}, u32[]{:S(2)}) copy-start(f32[1152]{0:T(1024)} %param.26) | copy-start | bytes 13828
  65.6 22.5 %copy-start.2 = (bf16[576,1152]{1,0:T(8,128)(2,1)S(1)}, bf16[576,1152]{1,0:T(8,128)(2,1)}, u32[]{:S(2)}) copy-start(bf16[576,1152]{1,0:T(8,128)(2,1)} %weight.3) | copy-start | bytes 3981316
  65.6 22.5 %copy-start.5 = (f32[1,96,128]{2,1,0:T(8,128)S(1)}, f32[1,96,128]{2,1,0:T(8,128)}, u32[]{:S(2)}) copy-start(f32[1,96,128]{2,1,0:T(8,128)} %param.15) | copy-start | bytes 147460
  65.6 22.5 %copy-start.6 = (bf16[1152,16]{0,1:T(8,128)(2,1)S(1)}, bf16[1152,16]{0,1:T(8,128)(2,1)}, u32[]{:S(2)}) copy-start(bf16[1152,16]{0,1:T(8,128)(2,1)} %param.27) | copy-start | bytes 110596
  75.1 26.8 %all-to-all-start = ((bf16[8,64,576]{2,1,0:T(8,128)(2,1)}), bf16[8,64,576]{2,1,0:T(8,128)(2,1)S(1)}, u32[]{:S(2)}, u32[]{:S(2)}) async-start(bf16[8,64,576]{2,1,0:T(8,128)(2,1)} %mix_frames.2), calls=%async_computation | async-start | bytes 1310720 | tf_op jit(solution)/shard_map/all_to_all | solution.py:592
  101.8 9.0 %copy-start.9 = (f32[96,128]{1,0:T(8,128)S(1)}, f32[96,128]{1,0:T(8,128)}, u32[]{:S(2)}) copy-start(f32[96,128]{1,0:T(8,128)} %param.16) | copy-start | bytes 147460
  105.7 5.1 %collective-permute-start.9 = (bf16[96,128]{1,0:T(8,128)(2,1)}, bf16[96,128]{1,0:T(8,128)(2,1)S(1)}, u32[]{:S(2)}, u32[]{:S(2)}) collective-permute-start(bf16[96,128]{1,0:T(8,128)(2,1)} %get-tuple-element.48), channel_id=1, source_target_pairs={{0,2},{2,4},{4,6},{6,8},{8,10},{10,12},{12,14},{1,3},{3,5},{5,7},{... | collective-permute-start | bytes 73736 | tf_op jit(solution)/shard_map/ppermute | solution.py:37
